TPU v7x, 32 devices: a whole 2x2x4 slice. The times are simulated.
32 devices in a mesh: tp: 4 (over z), ep: 8 (over y, x, core).
Axes of the slice: x: 2, y: 2, z: 4, core: 2. Of those that a mesh axis runs over, the one named last changes fastest.
Arguments:
- tokens: bfloat16 [3072, 2048], P('ep', 'tp'), may hold values from -6 to 6
- norm_gain: float32 [2048], replicated, may hold values from 0.25 to 1.75
- shared_gate: bfloat16 [2048, 2816], P('ep', 'tp'), may hold values from -0.125 to 0.125
- shared_up: bfloat16 [2048, 2816], P('ep', 'tp'), may hold values from -0.125 to 0.125
- shared_down: bfloat16 [2816, 2048], P('tp', 'ep'), may hold values from -0.15625 to 0.15625
- expert_gate: bfloat16 [4, 8, 704, 2048], P('tp', 'ep'), may hold values from -0.125 to 0.125
- expert_up: bfloat16 [4, 8, 704, 2048], P('tp', 'ep'), may hold values from -0.125 to 0.125
- expert_down: bfloat16 [16, 1408, 2048], P('ep', None, 'tp'), may hold values from -0.15625 to 0.15625
- chosen: int32 [16, 384], P('ep'), may hold values from 0 to 3071, as said below
- gates: float32 [16, 384], P('ep'), may hold values from 0.1 to 1
Outputs:
- mixed: bfloat16 [3072, 2048], P('ep', 'tp')
Inputs may be any that keep to these rules, and one draw needn't show every extreme that they name: Each row of chosen holds 384 different token indices in rising order. Of one row, at most 96 lie among the 384 tokens of one index of ep (tokens s * 384 to (s + 1) * 384 - 1), and in every row exactly 96 lie among those of some index.
All inputs are finite; a program needn't handle non-finite values.
Results may differ from a plain program's by a relative error of at most 0.012.
Values may be sent and summed in bfloat16 or wider, within the bound.
No kernel may reach another device: no remote copies, remote signals or barrier semaphores. Data moves between devices by JAX's collectives and lax.ppermute only.
A program may use at most 64 MiB of HBM per device.

v0:
```python
import jax
import jax.numpy as jnp
from jax import lax
from jax.sharding import PartitionSpec as P

EXP_DEV = 2
TOK_DEV = 384
CAP = 384


norm_eps = 1e-06


def on_device(
    tokens,
    norm_gain,
    shared_gate,
    shared_up,
    shared_down,
    expert_gate,
    expert_up,
    expert_down,
    chosen,
    gates,
):
    tp_count = lax.axis_size("tp")
    ep_count = lax.axis_size("ep")
    slice_width = tokens.shape[1]
    whole = lax.all_gather(tokens, "tp", axis=1, tiled=True)
    widened = whole.astype(jnp.float32)
    inv_scale = lax.rsqrt(jnp.mean(widened * widened, axis=1, keepdims=True) + norm_eps)
    normed = (widened * inv_scale * norm_gain).astype(jnp.bfloat16)
    gate_sum = jnp.dot(
        normed,
        lax.all_gather(shared_gate, "ep", axis=0, tiled=True),
        preferred_element_type=jnp.float32,
    )
    up_sum = jnp.dot(
        normed,
        lax.all_gather(shared_up, "ep", axis=0, tiled=True),
        preferred_element_type=jnp.float32,
    )
    shared_hidden = (jax.nn.silu(gate_sum) * up_sum).astype(jnp.bfloat16)
    partial_out = jnp.dot(
        shared_hidden,
        lax.all_gather(shared_down, "ep", axis=1, tiled=True),
        preferred_element_type=jnp.float32,
    )
    shared_part = lax.psum_scatter(partial_out, "tp", scatter_dimension=1, tiled=True)
    slot_most = 2 * CAP // ep_count
    slot_count = ep_count * slot_most
    sources = chosen // TOK_DEV
    source_flags = (
        sources[:, :, None] == jnp.arange(ep_count, dtype=jnp.int32)[None, None, :]
    ).astype(jnp.int32)
    counts = jnp.sum(source_flags, axis=1)
    starts = jnp.cumsum(counts, axis=1) - counts
    run_start = jnp.take_along_axis(starts, sources, axis=1)
    slot_index = sources * slot_most + jnp.arange(CAP, dtype=jnp.int32)[None, :] - run_start
    local_ids = chosen - sources * TOK_DEV
    expert_rows = jnp.arange(EXP_DEV, dtype=jnp.int32)[:, None]
    requests = (
        jnp.full((EXP_DEV, slot_count), TOK_DEV, jnp.int32)
        .at[expert_rows, slot_index]
        .set(local_ids)
    )
    requests = requests.reshape(EXP_DEV, ep_count, slot_most)
    asked_ids = lax.all_to_all(requests, "ep", split_axis=1, concat_axis=1, tiled=True)
    clipped = jnp.minimum(asked_ids, TOK_DEV - 1)
    local_expert = lax.axis_index("tp") // (tp_count // EXP_DEV)
    own_columns = lax.dynamic_slice_in_dim(
        normed, lax.axis_index("tp") * slice_width, slice_width, 1
    )
    outgoing = jnp.take(own_columns, clipped.reshape(-1), axis=0).reshape(
        EXP_DEV, ep_count, slot_most, slice_width
    )
    arrived = lax.all_to_all(outgoing, "ep", split_axis=1, concat_axis=1, tiled=True)
    copies = jnp.repeat(arrived, tp_count // EXP_DEV, axis=0)
    joined = lax.all_to_all(copies, "tp", split_axis=0, concat_axis=3, tiled=True)
    token_rows = joined.reshape(slot_count, -1)
    own_slots = lax.dynamic_index_in_dim(slot_index, local_expert, 0, keepdims=False)
    used_rows = jnp.take(token_rows, own_slots, axis=0)
    gate_weight = expert_gate.reshape(expert_gate.shape[2], expert_gate.shape[3])
    up_weight = expert_up.reshape(expert_up.shape[2], expert_up.shape[3])
    gate_values = jnp.einsum(
        "hd,rd->hr", gate_weight, used_rows, preferred_element_type=jnp.float32
    )
    up_values = jnp.einsum("hd,rd->hr", up_weight, used_rows, preferred_element_type=jnp.float32)
    part_hidden = (jax.nn.silu(gate_values) * up_values).astype(jnp.bfloat16)
    all_hidden = lax.all_gather(part_hidden, "tp", axis=0, tiled=True)
    width_hidden = expert_down.shape[1]
    placed_rows = []
    for expert_slot in range(EXP_DEV):
        hidden_block = all_hidden[expert_slot * width_hidden : (expert_slot + 1) * width_hidden, :]
        outputs = jnp.einsum(
            "fr,fd->rd", hidden_block, expert_down[expert_slot], preferred_element_type=jnp.float32
        )
        weighted = (gates[expert_slot][:, None] * outputs).astype(jnp.bfloat16)
        placed = (
            jnp.zeros((slot_count, slice_width), jnp.bfloat16)
            .at[slot_index[expert_slot]]
            .set(weighted)
        )
        placed_rows.append(placed)
    stacked = jnp.stack(placed_rows).reshape(EXP_DEV, ep_count, slot_most, slice_width)
    returned = lax.all_to_all(stacked, "ep", split_axis=1, concat_axis=1, tiled=True)
    flat_values = returned.reshape(-1, slice_width)
    flat_ids = asked_ids.reshape(-1)
    picker = (jnp.arange(TOK_DEV, dtype=jnp.int32)[:, None] == flat_ids[None, :]).astype(
        jnp.bfloat16
    )
    routed = jnp.dot(picker, flat_values, preferred_element_type=jnp.float32)
    return (shared_part + routed).astype(jnp.bfloat16)


def solution(mesh):
    return jax.shard_map(
        on_device,
        mesh=mesh,
        in_specs=(
            P("ep", "tp"),
            P(),
            P("ep", "tp"),
            P("ep", "tp"),
            P("tp", "ep"),
            P("tp", "ep", None, None),
            P("tp", "ep", None, None),
            P("ep", None, "tp"),
            P("ep", None),
            P("ep", None),
        ),
        out_specs=P("ep", "tp"),
        check_vma=False,
    )
```

profile of v0, /device:TPU:0, one launch (start us, length us, event | category | flops | bytes accessed | tf_op | source)
XLA Modules:
  0.0 314.7 jit_solution(7176182084578911614)
XLA Ops:
  6.5 0.7 all-gather.6.cloned.1.call-update
  8.7 0.7 multiply_subtract_fusion
  9.8 6.6 %gather_fusion.2 = s32[768]{0:T(1024)S(1)} fusion(s32[2,8]{1,0:T(2,128)S(1)} %sub.20, s32[768]{0:T(1024)S(1)} %reshape.205), kind=kCustom, calls=%fused_computation.2 | custom fusion | bytes 12288 | tf_op jit(solution)/shard_map/jit(take_along_axis)/gather | solution.py:58
  16.5 36.5 %scatter_fusion = s32[2,768]{1,0:T(2,128)S(1)} fusion(s32[2,768]{1,0:T(2,128)S(1)} %broadcast_in_dim.47, s32[768]{0:T(1024)S(1)} %reshape.211, s32[768]{0:T(1024)S(1)} %reshape.213), kind=kCustom, calls=%fused_computation.3 | custom fusion | bytes 15360 | tf_op jit(solution)/shard_map/scatter | solution.py:65
  53.7 5.2 %all-to-all-start = ((s32[2,8,96]{2,0,1:T(2,128)}), s32[2,8,96]{2,0,1:T(2,128)S(1)}, u32[]{:S(2)}, u32[]{:S(2)}) async-start(s32[2,8,96]{2,0,1:T(2,128)} %copy.24), calls=%async_computation.1 | async-start | bytes 16384 | tf_op jit(solution)/shard_map/all_to_all | solution.py:68
  58.9 4.9 %all-to-all-done = s32[2,8,96]{2,0,1:T(2,128)S(1)} async-done(((s32[2,8,96]{2,0,1:T(2,128)}), s32[2,8,96]{2,0,1:T(2,128)S(1)}, u32[]{:S(2)}, u32[]{:S(2)}) %all-to-all-start) | async-done | bytes 6176 | tf_op jit(solution)/shard_map/all_to_all | solution.py:68
  64.0 1.9 fusion
  66.4 1.2 copy-done.2
  67.6 5.4 %gather_fusion = bf16[1536,512]{1,0:T(8,128)(2,1)} fusion(bf16[384,512]{1,0:T(8,128)(2,1)S(1)} %constant_dynamic-slice_fusion, s32[2048]{0:T(1024)S(1)} %pad_clamp_fusion), kind=kCustom, calls=%fused_computation | custom fusion | bytes 3151872 | tf_op jit(solution)/shard_map/jit(_take)/gather | solution.py:74
  73.0 1.7 copy_select_fusion
  74.7 27.2 %all_to_all.30 = bf16[2,8,96,512]{3,2,0,1:T(8,128)(2,1)S(1)} all-to-all(bf16[2,8,96,512]{3,2,0,1:T(8,128)(2,1)S(1)} %copy_select_fusion), channel_id=1, replica_groups=mesh['tp'=4,'ep'=8] {'ep'}, dimensions={1} | all-to-all | bytes 3145728 | tf_op jit(solution)/shard_map/all_to_all | solution.py:77
  102.1 2.1 broadcast_in_dim.54
  104.2 4.9 %all-to-all-start.2 = ((bf16[4,8,96,512]{3,2,1,0:T(8,128)(2,1)}), bf16[4,8,96,512]{3,2,1,0:T(8,128)(2,1)}, u32[]{:S(2)}, u32[]{:S(2)}) async-start(bf16[4,8,96,512]{3,2,1,0:T(8,128)(2,1)} %bitcast.74), calls=%async_computation.3 | async-start | bytes 6291456 | tf_op jit(solution)/shard_map/all_to_all | solution.py:79
  109.9 68.8 %all-to-all-done.2 = bf16[4,8,96,512]{3,2,1,0:T(8,128)(2,1)} async-done(((bf16[4,8,96,512]{3,2,1,0:T(8,128)(2,1)}), bf16[4,8,96,512]{3,2,1,0:T(8,128)(2,1)}, u32[]{:S(2)}, u32[]{:S(2)}) %all-to-all-start.2) | async-done | bytes 3145760 | tf_op jit(solution)/shard_map/all_to_all | solution.py:79
  178.7 4.3 %copy.29 = bf16[1,8,96,4,512]{4,3,2,1,0:T(4,128)(2,1)S(1)} copy(bf16[1,8,96,4,512]{4,2,1,3,0:T(8,128)(2,1)} %bitcast.6) | data formatting | bytes 6291456 | tf_op jit(solution)/shard_map/all_to_all | solution.py:79
  183.1 2.7 copy.31
  185.8 7.3 %gather_fusion.1 = bf16[384,2048]{1,0:T(8,128)(2,1)} fusion(bf16[768,2048]{1,0:T(8,128)(2,1)} %bitcast.73, s32[1024]{0:T(1024)S(1)} %pad_clamp_fusion.1), kind=kCustom, calls=%fused_computation.1 | custom fusion | bytes 3147264 | tf_op jit(solution)/shard_map/jit(_take)/gather | solution.py:82
  193.1 3.3 %fusion.14 = f32[704,384]{1,0:T(8,128)S(1)} fusion(bf16[1,1,704,2048]{3,2,1,0:T(8,128)(2,1)S(1)} %copy-done, bf16[384,2048]{1,0:T(8,128)(2,1)} %gather_fusion.1, pred[384]{0:T(512)(128)(4,1)S(1)} %compare_and_fusion.1), kind=kOutput, calls=%fused_computation.26 | convolution fusion | flops 1108082688 | bytes 5538176 | tf_op jit(solution)/shard_map/hd,rd->hr/dot_general | solution.py:85
  196.5 2.6 fusion.24
  199.4 4.9 %fusion.63 = f32[384,704]{0,1:T(8,128)} fusion(bf16[384,2048]{1,0:T(8,128)(2,1)} %copy-done.2, bf16[2048,704]{0,1:T(8,128)(2,1)} %all-gather.8.cloned.1.call-done), kind=kOutput, calls=%fused_computation.87 | convolution fusion | flops 1107296256 | bytes 5537792 | tf_op jit(solution)/shard_map/dot_general | solution.py:33
  204.4 8.4 %fusion.44 = f32[384,2048]{1,0:T(8,128)} fusion(bf16[704,2048]{1,0:T(8,128)(2,1)} %all-gather.12.cloned.1.call-done, bf16[384,2048]{1,0:T(8,128)(2,1)} %copy-done.2, bf16[2048,704]{0,1:T(8,128)(2,1)} %all-gather.10.cloned.1.call-done, f32[384,704]{0,1:T(8,128)} %fusion.63), kind=kOutput, calls=%fused_computation.41 | convolution fusion | flops 2216214528 | bytes 11567104 | tf_op jit(solution)/shard_map/dot_general | solution.py:44
  213.5 29.9 %all-gather.14.cloned.1.call-done = bf16[2816,384]{1,0:T(8,128)(2,1)} async-done(((bf16[704,384]{1,0:T(8,128)(2,1)}), bf16[2816,384]{1,0:T(8,128)(2,1)}) %all-gather.14.cloned.1.call-update) | async-done | bytes 2162704 | tf_op jit(solution)/shard_map/all_gather | solution.py:90
  243.3 3.2 %fusion.35 = bf16[384,512]{1,0:T(8,128)(2,1)} fusion(bf16[2,1408,512]{2,1,0:T(8,128)(2,1)} %param.17, bf16[2816,384]{1,0:T(8,128)(2,1)} %all-gather.14.cloned.1.call-done, f32[384]{0:T(512)S(1)} %get-tuple-element.6), kind=kOutput, calls=%fused_computation.36 | convolution fusion | flops 554041344 | bytes 2917888 | tf_op jit(solution)/shard_map/fr,fd->rd/dot_general | solution.py:95
  246.6 3.3 %scatter_custom_fusion.2 = bf16[768,512]{1,0:T(8,128)(2,1)} fusion(s32[384]{0:T(512)S(1)} %get-tuple-element.9, bf16[384,512]{1,0:T(8,128)(2,1)} %fusion.35, bf16[]{:T(256)} %constant.101.clone.1), kind=kCustom, calls=%fused_computation.43 | custom fusion | bytes 786944 | tf_op jit(solution)/shard_map/scatter | solution.py:102
  249.9 3.5 %fusion.38 = bf16[384,512]{1,0:T(8,128)(2,1)} fusion(bf16[2,1408,512]{2,1,0:T(8,128)(2,1)} %param.17, bf16[2816,384]{1,0:T(8,128)(2,1)} %all-gather.14.cloned.1.call-done, f32[384]{0:T(512)S(1)} %get-tuple-element.5), kind=kOutput, calls=%fused_computation.37 | convolution fusion | flops 554041344 | bytes 2917888 | tf_op jit(solution)/shard_map/fr,fd->rd/dot_general | solution.py:95
  253.4 3.4 %scatter_custom_fusion.1 = bf16[768,512]{1,0:T(8,128)(2,1)} fusion(s32[384]{0:T(512)S(1)} %get-tuple-element.7, bf16[384,512]{1,0:T(8,128)(2,1)} %fusion.38, bf16[]{:T(256)} %constant.101.clone.1), kind=kCustom, calls=%fused_computation.45 | custom fusion | bytes 786944 | tf_op jit(solution)/shard_map/scatter | solution.py:102
  256.8 2.7 pad_maximum_fusion
  259.5 4.3 %all-to-all-start.3 = ((bf16[2,8,96,512]{3,2,0,1:T(8,128)(2,1)}), bf16[2,8,96,512]{3,2,0,1:T(8,128)(2,1)}, u32[]{:S(2)}, u32[]{:S(2)}) async-start(bf16[2,8,96,512]{3,2,0,1:T(8,128)(2,1)} %pad_maximum_fusion), calls=%async_computation.4 | async-start | bytes 3145728 | tf_op jit(solution)/shard_map/all_to_all | solution.py:106
  263.9 20.9 %all-to-all-done.3 = bf16[2,8,96,512]{3,2,0,1:T(8,128)(2,1)} async-done(((bf16[2,8,96,512]{3,2,0,1:T(8,128)(2,1)}), bf16[2,8,96,512]{3,2,0,1:T(8,128)(2,1)}, u32[]{:S(2)}, u32[]{:S(2)}) %all-to-all-start.3) | async-done | bytes 1572896 | tf_op jit(solution)/shard_map/all_to_all | solution.py:106
  284.8 2.8 copy.30
  287.5 17.2 %reduce-scatter.2.cloned.1.call-done = f32[384,512]{1,0:T(8,128)} async-done(((f32[384,2048]{1,0:T(8,128)}), f32[384,512]{1,0:T(8,128)}) %reduce-scatter.2.cloned.1.call-update) | async-done | bytes 786448 | tf_op jit(solution)/shard_map/reduce_scatter | solution.py:49
  304.7 3.1 fusion.34
  (57 shorter events, 5.2 us)
Async XLA Ops:
  6.5 186.6 %copy-start = (bf16[1,1,704,2048]{3,2,1,0:T(8,128)(2,1)S(1)}, bf16[1,1,704,2048]{3,2,1,0:T(8,128)(2,1)}, u32[]{:S(2)}) copy-start(bf16[1,1,704,2048]{3,2,1,0:T(8,128)(2,1)} %param.15) | copy-start | bytes 8650756
  6.5 57.5 %all-gather.6.cloned.1.call-start = ((), (), s32[]{:S(2)}) async-start(), calls=%async_computation.5 | async-start | bytes 1966080 | tf_op jit(solution)/shard_map/all_gather | solution.py:29
  7.3 192.1 %all-gather.8.cloned.1.call-start = ((), (), s32[]{:S(2)}) async-start(), calls=%async_computation.6 | async-start | bytes 3244032 | tf_op jit(solution)/shard_map/all_gather | solution.py:35
  8.0 196.3 %all-gather.12.cloned.1.call-start = ((), (), s32[]{:S(2)}) async-start(), calls=%async_computation.8 | async-start | bytes 3244032 | tf_op jit(solution)/shard_map/all_gather | solution.py:46
  53.0 13.0 %copy-start.4 = (f32[2048]{0:T(1024)S(1)}, f32[2048]{0:T(1024)}, u32[]{:S(2)}) copy-start(f32[2048]{0:T(1024)} %param.11) | copy-start | bytes 24580
  53.7 10.1 %all-to-all-start = ((s32[2,8,96]{2,0,1:T(2,128)}), s32[2,8,96]{2,0,1:T(2,128)S(1)}, u32[]{:S(2)}, u32[]{:S(2)}) async-start(s32[2,8,96]{2,0,1:T(2,128)} %copy.24), calls=%async_computation.1 | async-start | bytes 16384 | tf_op jit(solution)/shard_map/all_to_all | solution.py:68
  64.0 1.9 copy-start.1
  66.4 1.2 copy-start.2
  104.2 74.6 %all-to-all-start.2 = ((bf16[4,8,96,512]{3,2,1,0:T(8,128)(2,1)}), bf16[4,8,96,512]{3,2,1,0:T(8,128)(2,1)}, u32[]{:S(2)}, u32[]{:S(2)}) async-start(bf16[4,8,96,512]{3,2,1,0:T(8,128)(2,1)} %bitcast.74), calls=%async_computation.3 | async-start | bytes 6291456 | tf_op jit(solution)/shard_map/all_to_all | solution.py:79
  109.0 95.3 %all-gather.10.cloned.1.call-start = ((), (), s32[]{:S(2)}) async-start(), calls=%async_computation.7 | async-start | bytes 3244032 | tf_op jit(solution)/shard_map/all_gather | solution.py:40
  109.6 133.7 %all-gather.14.cloned.1.call-start = ((), (), s32[]{:S(2)}) async-start(), calls=%async_computation.10 | async-start | bytes 2703360 | tf_op jit(solution)/shard_map/all_gather | solution.py:90
  193.1 3.3 %copy-start.3 = (bf16[384,2048]{1,0:T(8,128)(2,1)S(1)}, bf16[384,2048]{1,0:T(8,128)(2,1)}, u32[]{:S(2)}) copy-start(bf16[384,2048]{1,0:T(8,128)(2,1)} %gather_fusion.1) | copy-start | bytes 4718596
  193.1 3.3 %copy-start.6 = (bf16[1,1,704,2048]{3,2,1,0:T(8,128)(2,1)S(1)}, bf16[1,1,704,2048]{3,2,1,0:T(8,128)(2,1)}, u32[]{:S(2)}) copy-start(bf16[1,1,704,2048]{3,2,1,0:T(8,128)(2,1)} %param.16) | copy-start | bytes 8650756
  199.1 105.6 %reduce-scatter.2.cloned.1.call-start = ((), (), s32[]{:S(2)}) async-start(), calls=%async_computation.9 | async-start | bytes 3932160 | tf_op jit(solution)/shard_map/reduce_scatter | solution.py:49
  212.8 0.7 copy-start.5
  259.5 25.3 %all-to-all-start.3 = ((bf16[2,8,96,512]{3,2,0,1:T(8,128)(2,1)}), bf16[2,8,96,512]{3,2,0,1:T(8,128)(2,1)}, u32[]{:S(2)}, u32[]{:S(2)}) async-start(bf16[2,8,96,512]{3,2,0,1:T(8,128)(2,1)} %pad_maximum_fusion), calls=%async_computation.4 | async-start | bytes 3145728 | tf_op jit(solution)/shard_map/all_to_all | solution.py:106
Sparse Core Ops, SparseCore 0:
  8.9 39.7 all-gather.5
  50.6 30.5 all-gather.7
  83.0 35.6 all-gather.11
  120.5 31.5 all-gather.9
  199.2 44.0 all-gather.13
  245.5 59.1 reduce-scatter.1
where the time goes:
time: 315 us
  waiting for transfers between devices  144 us (46%)
  local copies, waits for them, and re-layouts  77.4 us (25%)
  matrix products  29.2 us (9%)
  blocking collectives  27.2 us (9%)
  starting transfers between devices  14.9 us (5%)
  between operations  13.7 us (4%)
  other arithmetic  7.88 us (3%)
    all_to_all x1, waiting for transfers between devices, on_device(): lax.all_to_all(copies, 'tp', split_axis=0, concat_axis=3, tiled=True)  68.8 us
    scatter x1, local copies, waits for them, and re-layouts, on_device(): requests = jnp.full((EXP_DEV, slot_count), TOK_DEV, jnp.int32).at[expert_...  36.5 us
    all_gather x1, waiting for transfers between devices, on_device(): all_hidden = lax.all_gather(part_hidden, 'tp', axis=0, tiled=True)  29.9 us
    all_to_all x1, blocking collectives, on_device(): lax.all_to_all(outgoing, 'ep', split_axis=1, concat_axis=1, tiled=True)  27.2 us
    all_to_all x1, waiting for transfers between devices, on_device(): lax.all_to_all(stacked, 'ep', split_axis=1, concat_axis=1, tiled=True)  20.9 us
    reduce_scatter x1, waiting for transfers between devices, on_device(): lax.psum_scatter(partial_out, 'tp', scatter_dimension=1, tiled=True)  17.2 us
    dot_general x1, matrix products, on_device(): jnp.dot(shared_hidden, lax.all_gather(shared_down, 'ep', axis=1, tiled=Tr...  8.41 us
    gather x1, local copies, waits for them, and re-layouts, on_device(): used_rows = jnp.take(token_rows, own_slots, axis=0)  7.34 us
  transfers between devices with their start and end apart: 9, of which 5 were waited for; matrix products, arithmetic and copies ran while one was open for 35% of the time, Pallas kernels for 0%

commit v1 on v0

v1 whole, which is shorter than its diff:
```python
import jax
import jax.numpy as jnp
from jax import lax
from jax.experimental import pallas as pl
from jax.experimental.pallas import tpu as pltpu
from jax.sharding import PartitionSpec as P


norm_eps = 1e-06
F32 = jnp.float32
BF16 = jnp.bfloat16
MIB = 1 << 20


VMEM_SPEC = pl.BlockSpec(memory_space=pltpu.VMEM)
SMEM_SPEC = pl.BlockSpec(memory_space=pltpu.SMEM)
HBM_SPEC = pl.BlockSpec(memory_space=pltpu.HBM)


def swap(x, axis, mask):
    count = lax.axis_size(axis)
    return lax.ppermute(x, axis, [(i, i ^ mask) for i in range(count)])


def line_gather(near, far, axis):
    pair = lax.ppermute(near, axis, [(0, 1), (1, 0), (2, 3), (3, 2)])
    middle = lax.ppermute(far, axis, [(1, 2), (2, 1)])
    ends = lax.ppermute(far, axis, [(0, 2), (3, 1)])
    relay_middle = lax.ppermute(middle, axis, [(2, 3), (1, 0)])
    outer = lax.ppermute(far, axis, [(0, 3), (3, 0)])
    return [
        ([near], 0),
        ([pair], 1),
        ([ends, relay_middle], 2),
        ([middle, outer], 3),
    ]


def line_scatter(blocks, axis):
    one, two, three = blocks
    middle = lax.ppermute(three, axis, [(1, 2), (2, 1)])
    inward = lax.ppermute(two, axis, [(0, 2), (3, 1)])
    pair = swap(one, axis, 1)
    outward = lax.ppermute(two, axis, [(2, 0), (1, 3)])
    ends = lax.ppermute(three, axis, [(0, 3), (3, 0)])
    return [([pair], 1), ([inward, outward], 2), ([middle, ends], 3)]


def box_gather(x, axis, relay):
    near = {2: swap(x, axis, 2), 4: swap(x, axis, 4)}
    diagonal = swap(near.get(6 - relay, x), axis, relay)
    pieces = [(x, 0), (near[2], 2), (near[4], 4)]
    pieces += [(swap(a, axis, 1), m ^ 1) for a, m in pieces]
    pieces += [(diagonal, 6), (swap(diagonal, axis, 1), 7)]
    return [([a], m) for a, m in pieces]


def arrays_of(pieces):
    return [a for arrays, _ in pieces for a in arrays]


def read_piece(arrays, refs, at, flag):
    if len(arrays) == 1:
        return refs[at][...]
    return jnp.where(flag != 0, refs[at][...], refs[at + 1][...])


def copy_pieces(pieces, refs, flag, pos_ref, slot, target, dim):
    at = 0
    for number, (arrays, _) in enumerate(pieces):
        value = read_piece(arrays, refs, at, flag)
        at += len(arrays)
        if len(pieces) == 1:
            target[...] = value
        elif dim == 0:
            row = pl.multiple_of(pos_ref[slot + number], 64)
            target[pl.ds(row, value.shape[0]), :] = value
        else:
            col = pl.multiple_of(pos_ref[slot + number], 128)
            target[:, pl.ds(col, value.shape[1])] = value


def stack_scalars(values):
    return jnp.stack([jnp.asarray(v, jnp.int32) for v in values])


def silu(v):
    return v / (1.0 + jnp.exp(-v))


def normalise(x_ref, gain_ref):
    wide = x_ref[...].astype(F32)
    scale = lax.rsqrt(jnp.mean(wide * wide, axis=1, keepdims=True) + norm_eps)
    x_ref[...] = (wide * scale * gain_ref[...]).astype(BF16)


def dot(a, b, dims):
    return lax.dot_general(a, b, (dims, ((), ())), preferred_element_type=F32)


def one_hot(ids, shape, dim):
    span = lax.broadcasted_iota(jnp.int32, shape, dim)
    return jnp.where(ids == span, 1.0, 0.0).astype(BF16)


def kernel(body, out_shape, in_specs, scratch_shapes):
    outs = len(out_shape) if isinstance(out_shape, list) else None
    return pl.pallas_call(
        body,
        out_shape=out_shape,
        in_specs=in_specs,
        out_specs=VMEM_SPEC if outs is None else [VMEM_SPEC] * outs,
        scratch_shapes=scratch_shapes,
        compiler_params=pltpu.CompilerParams(vmem_limit_bytes=60 * MIB),
    )


def take_windows(pieces, flag, ids_column):
    arrays = arrays_of(pieces)
    tok_dev, width = arrays[0].shape
    slots = ids_column.shape[0]

    def body(pos_ref, ids_ref, *refs):
        picker = one_hot(ids_ref[...], (slots, tok_dev), 1)
        at = 0
        for number, (alternatives, _) in enumerate(pieces):
            value = read_piece(alternatives, refs, at, pos_ref[0])
            at += len(alternatives)
            rows = dot(picker, value, ((1,), (0,))).astype(BF16)
            refs[-1][:, number * width : (number + 1) * width] = rows

    return kernel(
        body,
        jax.ShapeDtypeStruct((slots, width * len(pieces)), BF16),
        [SMEM_SPEC] + [VMEM_SPEC] * (1 + len(arrays)),
        [],
    )(flag, ids_column, *arrays)


def expert_hidden(windows, width, positions, slot_lanes, gain, gate, up, cap):
    hidden, features = gate.shape

    def body(pos_ref, slot_ref, gain_ref, gate_hbm, up_hbm, *refs):
        out_ref, x_ref, gate_ref, up_ref, sems = refs[len(windows) :]
        gate_copy = pltpu.make_async_copy(gate_hbm, gate_ref, sems.at[0])
        up_copy = pltpu.make_async_copy(up_hbm, up_ref, sems.at[1])
        gate_copy.start()
        up_copy.start()
        picker = one_hot(slot_ref[...], (cap, slot_ref.shape[1]), 0)
        for number in range(len(windows)):
            rows = dot(picker, refs[number][...], ((1,), (0,))).astype(BF16)
            for part in range(rows.shape[1] // width):
                at = 1 + number * (rows.shape[1] // width) + part
                col = pl.multiple_of(pos_ref[at], 128)
                x_ref[:, pl.ds(col, width)] = rows[:, part * width : (part + 1) * width]
        normalise(x_ref, gain_ref)
        gate_copy.wait()
        gates = dot(gate_ref[...], x_ref[...], ((1,), (1,)))
        up_copy.wait()
        ups = dot(up_ref[...], x_ref[...], ((1,), (1,)))
        out_ref[...] = (silu(gates) * ups).astype(BF16)

    return kernel(
        body,
        jax.ShapeDtypeStruct((hidden, cap), BF16),
        [SMEM_SPEC, VMEM_SPEC, VMEM_SPEC, HBM_SPEC, HBM_SPEC] + [VMEM_SPEC] * len(windows),
        [
            pltpu.VMEM((cap, features), BF16),
            pltpu.VMEM((hidden, features), BF16),
            pltpu.VMEM((hidden, features), BF16),
            pltpu.SemaphoreType.DMA((2,)),
        ],
    )(positions, slot_lanes, gain, gate, up, *windows)


def expert_down(hidden_pieces, positions, down, gate_column, slot_rows):
    hidden, width = down.shape
    cap = gate_column.shape[0]
    slots = slot_rows.shape[0]
    arrays = arrays_of(hidden_pieces)

    def body(pos_ref, gate_ref, slot_ref, down_ref, *refs):
        out_ref, hidden_ref = refs[len(arrays) :]
        copy_pieces(hidden_pieces, refs, pos_ref[0], pos_ref, 1, hidden_ref, 0)
        out = dot(hidden_ref[...], down_ref[...], ((0,), (0,)))
        weighted = (gate_ref[...] * out).astype(BF16)
        picker = one_hot(slot_ref[...], (slots, cap), 1)
        out_ref[...] = dot(picker, weighted, ((1,), (0,))).astype(BF16)

    return kernel(
        body,
        jax.ShapeDtypeStruct((slots, width), BF16),
        [SMEM_SPEC] + [VMEM_SPEC] * (3 + len(arrays)),
        [pltpu.VMEM((hidden, cap), BF16)],
    )(positions, gate_column, slot_rows, down, *arrays)


def add_products(x_ref, total_ref, weights, positions, first):
    for number, (weight, col) in enumerate(zip(weights, positions)):
        x = x_ref[:, pl.ds(pl.multiple_of(col, 128), weight.shape[1])]
        part = dot(x, weight[...], ((1,), (1,)))
        if first and number == 0:
            total_ref[...] = part
        else:
            total_ref[...] += part


def shared_in(token_pieces, gates, ups, positions, gain):
    token_arrays = arrays_of(token_pieces)
    gate_arrays, up_arrays = arrays_of(gates), arrays_of(ups)
    tok_dev = token_arrays[0].shape[0]
    features = gain.shape[1]
    hidden = gate_arrays[0].shape[0]
    ends = [len(token_arrays), len(token_arrays) + len(gate_arrays)]
    count = ends[1] + len(up_arrays)

    def body(pos_ref, gain_ref, *refs):
        x_ref, gate_sum, up_sum = refs[count:]
        copy_pieces(token_pieces, refs, pos_ref[0], pos_ref, 1, x_ref, 1)
        normalise(x_ref, gain_ref)
        at = [pos_ref[1 + n] for n in range(count)]
        add_products(x_ref, gate_sum, refs[ends[0] : ends[1]], at[ends[0] : ends[1]], True)
        add_products(x_ref, up_sum, refs[ends[1] : count], at[ends[1] :], True)

    return kernel(
        body,
        [
            jax.ShapeDtypeStruct((tok_dev, features), BF16),
            jax.ShapeDtypeStruct((tok_dev, hidden), F32),
            jax.ShapeDtypeStruct((tok_dev, hidden), F32),
        ],
        [SMEM_SPEC] + [VMEM_SPEC] * (1 + count),
        [],
    )(positions, gain, *token_arrays, *gate_arrays, *up_arrays)


def shared_out(begun, gates, ups, downs, positions, width, blocks):
    arrays = arrays_of(gates) + arrays_of(ups) + arrays_of(downs)
    ends = [len(gates), len(gates) + len(ups)]
    count = len(arrays)
    tok_dev, features = begun[0].shape
    hidden = begun[1].shape[1]
    block = arrays[-1].shape[1]

    def body(pos_ref, x_ref, gate_in, up_in, *refs):
        outs = refs[count : count + blocks]
        gate_sum, up_sum, sum_ref = refs[count + blocks :]
        at = [pos_ref[n] for n in range(count)]
        gate_sum[...] = gate_in[...]
        add_products(x_ref, gate_sum, refs[: ends[0]], at[: ends[0]], False)
        up_sum[...] = up_in[...]
        add_products(x_ref, up_sum, refs[ends[0] : ends[1]], at[ends[0] : ends[1]], False)
        mid = (silu(gate_sum[...]) * up_sum[...]).astype(BF16)
        for number in range(ends[1], count):
            col = pl.multiple_of(at[number], 128)
            sum_ref[:, pl.ds(col, block)] = dot(mid, refs[number][...], ((1,), (0,)))
        for number in range(blocks):
            col = pl.multiple_of(pos_ref[count + number], 128)
            outs[number][...] = sum_ref[:, pl.ds(col, width)].astype(outs[number].dtype)

    return kernel(
        body,
        [
            jax.ShapeDtypeStruct((tok_dev, width), F32 if n == 0 else BF16)
            for n in range(blocks)
        ],
        [SMEM_SPEC] + [VMEM_SPEC] * (3 + count),
        [
            pltpu.VMEM((tok_dev, hidden), F32),
            pltpu.VMEM((tok_dev, hidden), F32),
            pltpu.VMEM((tok_dev, features), F32),
        ],
    )(positions, *begun, *arrays)


def finish(shared_own, shared_parts, windows, ids, flag, tok_dev):
    width = shared_own.shape[1]
    arrays = arrays_of(shared_parts)
    parts = len(arrays)

    def body(pos_ref, own_ref, *refs):
        total = own_ref[...]
        at = 0
        for alternatives, _ in shared_parts:
            total = total + read_piece(alternatives, refs, at, pos_ref[0]).astype(F32)
            at += len(alternatives)
        for number in range(len(windows)):
            values, id_ref = refs[parts + number], refs[parts + len(windows) + number]
            picker = one_hot(id_ref[...], (tok_dev, values.shape[0]), 0)
            total = total + dot(picker, values[...], ((1,), (0,)))
        refs[-1][...] = total.astype(BF16)

    return kernel(
        body,
        jax.ShapeDtypeStruct((tok_dev, width), BF16),
        [SMEM_SPEC] + [VMEM_SPEC] * (1 + parts + 2 * len(windows)),
        [],
    )(flag, shared_own, *arrays, *windows, *ids)


def on_device(
    tokens,
    norm_gain,
    shared_gate,
    shared_up,
    shared_down,
    expert_gate,
    expert_up,
    expert_down_weight,
    chosen,
    gates,
):
    tp_count = lax.axis_size("tp")
    ep_count = lax.axis_size("ep")
    tp = lax.axis_index("tp").astype(jnp.int32)
    ep = lax.axis_index("ep").astype(jnp.int32)
    tok_dev, width = tokens.shape
    experts, cap = chosen.shape
    split = tp_count // experts
    on_line = tp_count == 4 and experts == 2
    on_box = ep_count == 8
    inner = ((tp == 1) | (tp == 2)).astype(jnp.int32)
    gain = norm_gain[None, :]
    gate_weight = expert_gate.reshape(expert_gate.shape[2], expert_gate.shape[3])
    up_weight = expert_up.reshape(expert_up.shape[2], expert_up.shape[3])

    own_expert = tp // split
    order = [own_expert, 1 - own_expert]
    chosen_of = [lax.dynamic_index_in_dim(chosen, k, 0, keepdims=False) for k in order]
    gates_of = [lax.dynamic_index_in_dim(gates, k, 0, keepdims=False) for k in order]
    down_of = [
        lax.dynamic_index_in_dim(expert_down_weight, k, 0, keepdims=False) for k in order
    ]

    if on_line:
        token_pieces = [([tokens], 0)]
        token_pieces += [([swap(tokens, "tp", m)], m) for m in (1, 2, 3)]
    else:
        token_pieces = [([lax.all_gather(tokens, "tp", axis=1, tiled=True)], 0)]

    def gathered(weight, relay):
        if on_box:
            return box_gather(weight, "ep", relay)
        return [([lax.all_gather(weight, "ep", axis=1, tiled=True)], 0)]

    block = shared_down.shape[1]
    shared_gates = gathered(shared_gate.T, 2)
    shared_ups = gathered(shared_up.T, 6)
    shared_downs = gathered(shared_down, 4)

    window = 2 * cap // ep_count
    owner_start = jnp.arange(ep_count, dtype=jnp.int32) * tok_dev
    offsets = jnp.arange(window, dtype=jnp.int32)
    slot_rows = []
    slot_ids = []
    for ids in chosen_of:
        starts = jnp.sum((ids[None, :] < owner_start[:, None]).astype(jnp.int32), axis=1)
        rows = (starts[:, None] + offsets[None, :]).reshape(-1)
        slot_rows.append(rows.reshape(-1, 1))
        hit = rows[:, None] == jnp.arange(cap, dtype=jnp.int32)[None, :]
        found = jnp.sum(jnp.where(hit, ids[None, :] + 1, 0), axis=1) - 1
        slot_ids.append(found.reshape(ep_count, window) - owner_start[:, None])
    sent_ids = jnp.stack(slot_ids, axis=1)
    owner_ids = lax.all_to_all(sent_ids, "ep", split_axis=0, concat_axis=0, tiled=True)
    owner_ids = [owner_ids[:, k].reshape(1, -1) for k in range(experts)]

    feature_at = [inner] + [(tp ^ m) * width for _, m in token_pieces]
    flag = stack_scalars([inner])
    ids_column = owner_ids[0].reshape(-1, 1)
    arrived = []
    arrived_at = [inner]
    for number in range(0, len(token_pieces), 2):
        batch = token_pieces[number : number + 2]
        sent = take_windows(batch, flag, ids_column)
        sent = sent.reshape(ep_count, window, -1)
        rows = lax.all_to_all(sent, "ep", split_axis=0, concat_axis=0, tiled=True)
        arrived.append(rows.reshape(ep_count * window, -1))
        arrived_at += [(tp ^ mask) * width for _, mask in batch]
    piece_width = width if on_line else width * tp_count
    if not on_line:
        arrived_at = [inner, 0]
    part_hidden = expert_hidden(
        arrived,
        piece_width,
        stack_scalars(arrived_at),
        slot_rows[0].reshape(1, -1),
        gain,
        gate_weight,
        up_weight,
        cap,
    )

    hidden_rows = part_hidden.shape[0]
    if on_line:
        pieces = line_gather(part_hidden, part_hidden, "tp")
        hidden_of = [pieces[:2], pieces[2:]]
    else:
        whole = lax.all_gather(part_hidden, "tp", axis=0, tiled=True)
        units = hidden_rows * split
        hidden_of = [
            [([lax.dynamic_slice_in_dim(whole, k * units, units, 0)], 0)] for k in order
        ]

    def places(pieces):
        return [(ep ^ m) * block if on_box else 0 for _, m in pieces]

    early_gates, early_ups = shared_gates[:6], shared_ups[:6]
    late_gates, late_ups = shared_gates[6:], shared_ups[6:]
    in_at = feature_at + places(early_gates + early_ups)
    begun = shared_in(token_pieces, early_gates, early_ups, stack_scalars(in_at), gain)
    masks = [0, 1, 2, 3] if on_line else [0]
    out_at = places(late_gates + late_ups + shared_downs)
    out_at += [(tp ^ m) * width for m in masks] if on_line else [0]
    sums = shared_out(
        begun,
        late_gates,
        late_ups,
        shared_downs,
        stack_scalars(out_at),
        width if on_line else width * tp_count,
        len(masks),
    )
    if on_line:
        shared_own = sums[0]
        shared_parts = line_scatter(sums[1:], "tp")
    else:
        shared_own = lax.psum_scatter(sums[0], "tp", scatter_dimension=1, tiled=True)
        shared_parts = []

    windows = []
    for k in range(experts):
        hidden_at = [inner] + [((tp ^ m) % split) * hidden_rows for _, m in hidden_of[k]]
        sent = expert_down(
            hidden_of[k],
            stack_scalars(hidden_at),
            down_of[k],
            gates_of[k].reshape(-1, 1),
            slot_rows[k],
        )
        windows.append(lax.all_to_all(sent, "ep", split_axis=0, concat_axis=0, tiled=True))
    return finish(shared_own, shared_parts, windows, owner_ids, flag, tok_dev)


def solution(mesh):
    return jax.shard_map(
        on_device,
        mesh=mesh,
        in_specs=(
            P("ep", "tp"),
            P(),
            P("ep", "tp"),
            P("ep", "tp"),
            P("tp", "ep"),
            P("tp", "ep", None, None),
            P("tp", "ep", None, None),
            P("ep", None, "tp"),
            P("ep", None),
            P("ep", None),
        ),
        out_specs=P("ep", "tp"),
        check_vma=False,
    )
```

time: 315 us -> 248 us (0.79)
  the two profiles are of different devices: /device:TPU:0 before, /device:TPU:10 now
where the time goes in v1:
time: 248 us; the launch traced here: 247 us
  waiting for transfers between devices  118 us (48%)
  starting transfers between devices  66.2 us (27%)
  Pallas kernels  40.8 us (16%)
  local copies, waits for them, and re-layouts  17.7 us (7%)
  other arithmetic  3.75 us (2%)
    ppermute x25, waiting for transfers between devices, swap(): return lax.ppermute(x, axis, [(i, i ^ mask) for i in range(count)])  70.9 us
    ppermute x25, starting transfers between devices, swap(): return lax.ppermute(x, axis, [(i, i ^ mask) for i in range(count)])  18.3 us
    ppermute x1, waiting for transfers between devices, line_scatter(): outward = lax.ppermute(two, axis, [(2, 0), (1, 3)])  13.5 us
    ppermute x1, waiting for transfers between devices, line_gather(): relay_middle = lax.ppermute(middle, axis, [(2, 3), (1, 0)])  11.6 us
    all_to_all x2, starting transfers between devices, on_device(): rows = lax.all_to_all(sent, 'ep', split_axis=0, concat_axis=0, tiled=True)  9.31 us
    all_to_all x2, starting transfers between devices, on_device(): lax.all_to_all(sent, 'ep', split_axis=0, concat_axis=0, tiled=True)  9.28 us
    ppermute x1, waiting for transfers between devices, line_scatter(): middle = lax.ppermute(three, axis, [(1, 2), (2, 1)])  9.11 us
    pallas_call x2, Pallas kernels, expert_down(): kernel(body, jax.ShapeDtypeStruct((slots, width), BF16), [SMEM_SPEC] + [V...  8.73 us
  transfers between devices with their start and end apart: 39, of which 15 were waited for; matrix products, arithmetic and copies ran while one was open for 7% of the time, Pallas kernels for 14%

profile of v1, /device:TPU:10, one launch (start us, length us, event | category | flops | bytes accessed | tf_op | source)
XLA Modules:
  0.0 246.9 jit_solution(2161205437171952833)
XLA Ops:
  3.1 4.3 %all-to-all-start = ((s32[8,2,96]{2,1,0:T(2,128)}), s32[8,2,96]{2,1,0:T(2,128)S(1)}, u32[]{:S(2)}, u32[]{:S(2)}) async-start(s32[8,2,96]{2,1,0:T(2,128)} %pad_add_fusion), calls=%async_computation | async-start | bytes 16384 | tf_op jit(solution)/shard_map/all_to_all | solution.py:364
  7.4 3.3 %all-to-all-done = s32[8,2,96]{2,1,0:T(2,128)S(1)} async-done(((s32[8,2,96]{2,1,0:T(2,128)}), s32[8,2,96]{2,1,0:T(2,128)S(1)}, u32[]{:S(2)}, u32[]{:S(2)}) %all-to-all-start) | async-done | bytes 6176 | tf_op jit(solution)/shard_map/all_to_all | solution.py:364
  12.4 3.4 %shard_map.102 = bf16[768,1024]{1,0:T(8,128)(2,1)} custom-call(s32[1]{0:T(128)} %bitcast.pos_ref, s32[768,1]{1,0:T(8,128)} %reshape_reshape_squeeze.4.ids_ref, bf16[384,512]{1,0:T(8,128)(2,1)} %refs_0_.3, bf16[384,512]{1,0:T(8,128)(2,1)} %copy-done.6), custom_call_target="tpu_custom_call" | custom-call | tf_op jit(solution)/shard_map/pallas_call | solution.py:132
  15.9 5.1 %all-to-all-start.1 = ((bf16[8,96,1024]{2,1,0:T(8,128)(2,1)}), bf16[8,96,1024]{2,1,0:T(8,128)(2,1)S(1)}, u32[]{:S(2)}, u32[]{:S(2)}) async-start(bf16[8,96,1024]{2,1,0:T(8,128)(2,1)} %bitcast.42), calls=%async_computation.1 | async-start | bytes 3145728 | tf_op jit(solution)/shard_map/all_to_all | solution.py:376
  21.0 2.6 %collective-permute-start.1 = (bf16[384,512]{1,0:T(8,128)(2,1)S(1)}, bf16[384,512]{1,0:T(8,128)(2,1)S(1)}, u32[]{:S(2)}, u32[]{:S(2)}) collective-permute-start(bf16[384,512]{1,0:T(8,128)(2,1)S(1)} %copy-done.5), channel_id=1, source_target_pairs={{0,16},{8,24},{16,0},{24,8},{1,17},{9,25},{17,1},{25,9},{2,18},{10... | collective-permute-start | bytes 1179656 | tf_op jit(solution)/shard_map/ppermute | solution.py:22
  24.0 25.9 %collective-permute-done.1.refs_2_.refs_0_ = bf16[384,512]{1,0:T(8,128)(2,1)S(1)} collective-permute-done((bf16[384,512]{1,0:T(8,128)(2,1)S(1)}, bf16[384,512]{1,0:T(8,128)(2,1)S(1)}, u32[]{:S(2)}, u32[]{:S(2)}) %collective-permute-start.1) | collective-permute-done | bytes 393248 | tf_op jit(solution)/shard_map/ppermute | solution.py:22
  49.9 8.4 %collective-permute-done.2.refs_3_.refs_1_ = bf16[384,512]{1,0:T(8,128)(2,1)S(1)} collective-permute-done((bf16[384,512]{1,0:T(8,128)(2,1)S(1)}, bf16[384,512]{1,0:T(8,128)(2,1)S(1)}, u32[]{:S(2)}, u32[]{:S(2)}) %collective-permute-start.2) | collective-permute-done | bytes 393248 | tf_op jit(solution)/shard_map/ppermute | solution.py:22
  59.0 3.5 %shard_map.103 = bf16[768,1024]{1,0:T(8,128)(2,1)} custom-call(s32[1]{0:T(128)} %bitcast.pos_ref, s32[768,1]{1,0:T(8,128)} %reshape_reshape_squeeze.4.ids_ref, bf16[384,512]{1,0:T(8,128)(2,1)} %copy-done.7, bf16[384,512]{1,0:T(8,128)(2,1)} %copy-done.8), custom_call_target="tpu_custom_call" | custom-call | tf_op jit(solution)/shard_map/pallas_call | solution.py:132
  63.7 4.2 %all-to-all-start.2 = ((bf16[8,96,1024]{2,1,0:T(8,128)(2,1)}), bf16[8,96,1024]{2,1,0:T(8,128)(2,1)S(1)}, u32[]{:S(2)}, u32[]{:S(2)}) async-start(bf16[8,96,1024]{2,1,0:T(8,128)(2,1)} %bitcast.40), calls=%async_computation.2 | async-start | bytes 3145728 | tf_op jit(solution)/shard_map/all_to_all | solution.py:376
  72.0 22.5 %collective-permute-done.3.refs_5_ = bf16[704,256]{1,0:T(8,128)(2,1)} collective-permute-done((bf16[704,256]{1,0:T(8,128)(2,1)}, bf16[704,256]{1,0:T(8,128)(2,1)}, u32[]{:S(2)}, u32[]{:S(2)}) %collective-permute-start.3) | collective-permute-done | bytes 360480 | tf_op jit(solution)/shard_map/ppermute | solution.py:22
  95.3 2.1 collective-permute-start.15
  97.9 4.2 %collective-permute-done.8.refs_11_ = bf16[704,256]{1,0:T(8,128)(2,1)} collective-permute-done((bf16[704,256]{1,0:T(8,128)(2,1)}, bf16[704,256]{1,0:T(8,128)(2,1)}, u32[]{:S(2)}, u32[]{:S(2)}) %collective-permute-start.8) | collective-permute-done | bytes 360480 | tf_op jit(solution)/shard_map/ppermute | solution.py:22
  106.7 8.1 %shard_map.104.refs_0_ = bf16[704,384]{1,0:T(8,128)(2,1)} custom-call(s32[5]{0:T(128)} %stack.120.pos_ref, s32[1,768]{1,0:T(1,128)} %add.125.slot_ref, f32[1,2048]{1,0:T(1,128)} %bitcast.58, bf16[704,2048]{1,0:T(8,128)(2,1)} %bitcast.47, bf16[704,2048]{1,0:T(8,128)(2,1)} %bitcast.48, bf16[768,1024]{1,0:T(8,128)(2,1)} %bitcast.39, bf16[768,1024]{1,0:T(8,128)(2,1)} %bitcast.41), custom_call_target="tpu_custom_call" | custom-call | tf_op jit(solution)/shard_map/pallas_call | solution.py:163
  118.4 3.6 %collective-permute-start.31 = (bf16[704,384]{1,0:T(8,128)(2,1)}, bf16[704,384]{1,0:T(8,128)(2,1)S(1)}, u32[]{:S(2)}, u32[]{:S(2)}) collective-permute-start(bf16[704,384]{1,0:T(8,128)(2,1)} %shard_map.104.refs_0_), channel_id=1, source_target_pairs={{8,16},{16,8},{9,17},{17,9},{10,18},{18,10},{11,19},{19,11},{12,20... | collective-permute-start | bytes 1622024 | tf_op jit(solution)/shard_map/ppermute | solution.py:27
  122.0 3.6 %dynamic-slice_bitcast_fusion = (bf16[1408,512]{1,0:T(8,128)(2,1)}, bf16[1408,512]{1,0:T(8,128)(2,1)}) fusion(bf16[2,1408,512]{2,1,0:T(8,128)(2,1)} %param.17, s32[]{:T(128)S(6)} %select_n.48, s32[]{:T(128)S(6)} %select_n.46), kind=kLoop, calls=%fused_computation | loop fusion | bytes 5767176 | tf_op jit(solution)/shard_map/jit(dynamic_index_in_dim)/squeeze | solution.py:332
  125.6 2.3 collective-permute-done.29.refs_1_
  130.5 4.2 %shard_map.105 = bf16[768,512]{1,0:T(8,128)(2,1)} custom-call(s32[3]{0:T(128)} %pad_add_fusion.1.pos_ref, f32[384,1]{1,0:T(8,128)} %copy.25.gate_ref, s32[768,1]{1,0:T(8,128)} %add.137.slot_ref, bf16[1408,512]{1,0:T(8,128)(2,1)} %get-tuple-element.28.down_ref, bf16[704,384]{1,0:T(8,128)(2,1)} %shard_map.104.refs_0_, bf16[704,384]{1,0:T(8,128)(2,1)} %copy-done.13), custom_call_target="tpu_custom_call" | custom-call | tf_op jit(solution)/shard_map/pallas_call | solution.py:190
  134.7 5.0 %all-to-all-start.3 = ((bf16[8,96,512]{2,1,0:T(8,128)(2,1)}), bf16[8,96,512]{2,1,0:T(8,128)(2,1)S(1)}, u32[]{:S(2)}, u32[]{:S(2)}) async-start(bf16[8,96,512]{2,1,0:T(8,128)(2,1)} %bitcast.46), calls=%async_computation.3 | async-start | bytes 1572864 | tf_op jit(solution)/shard_map/all_to_all | solution.py:440
  141.8 8.4 %collective-permute-start.32 = (bf16[704,384]{1,0:T(8,128)(2,1)S(1)}, bf16[704,384]{1,0:T(8,128)(2,1)S(1)}, u32[]{:S(2)}, u32[]{:S(2)}) collective-permute-start(bf16[704,384]{1,0:T(8,128)(2,1)S(1)} %collective-permute-done.31.refs_2_), channel_id=1, source_target_pairs={{16,24},{8,0},{17,25},{9,1},{18,26},{10,2},{19,27},{11,3},{20,28},... | collective-permute-start | bytes 1622024 | tf_op jit(solution)/shard_map/ppermute | solution.py:29
  154.2 6.0 %collective-permute-done.13.refs_0_ = bf16[704,256]{1,0:T(8,128)(2,1)} collective-permute-done((bf16[704,256]{1,0:T(8,128)(2,1)}, bf16[704,256]{1,0:T(8,128)(2,1)}, u32[]{:S(2)}, u32[]{:S(2)}) %collective-permute-start.13) | collective-permute-done | bytes 360480 | tf_op jit(solution)/shard_map/ppermute | solution.py:22
  161.2 11.6 %collective-permute-done.32.refs_1_ = bf16[704,384]{1,0:T(8,128)(2,1)S(1)} collective-permute-done((bf16[704,384]{1,0:T(8,128)(2,1)S(1)}, bf16[704,384]{1,0:T(8,128)(2,1)S(1)}, u32[]{:S(2)}, u32[]{:S(2)}) %collective-permute-start.32) | collective-permute-done | bytes 540704 | tf_op jit(solution)/shard_map/ppermute | solution.py:29
  173.6 4.5 %shard_map.106 = bf16[768,512]{1,0:T(8,128)(2,1)} custom-call(s32[3]{0:T(128)} %pad_add_fusion.2.pos_ref, f32[384,1]{1,0:T(8,128)} %copy.27.gate_ref, s32[768,1]{1,0:T(8,128)} %add.138.slot_ref, bf16[1408,512]{1,0:T(8,128)(2,1)} %get-tuple-element.27.down_ref, bf16[704,384]{1,0:T(8,128)(2,1)} %copy-done.10, bf16[704,384]{1,0:T(8,128)(2,1)} %copy-done.12, ...), custom_call_target="tpu_custom_call" | custom-call | tf_op jit(solution)/shard_map/pallas_call | solution.py:190
  178.2 4.2 %all-to-all-start.4 = ((bf16[8,96,512]{2,1,0:T(8,128)(2,1)}), bf16[8,96,512]{2,1,0:T(8,128)(2,1)S(1)}, u32[]{:S(2)}, u32[]{:S(2)}) async-start(bf16[8,96,512]{2,1,0:T(8,128)(2,1)} %bitcast.43), calls=%async_computation.4 | async-start | bytes 1572864 | tf_op jit(solution)/shard_map/all_to_all | solution.py:440
  183.7 6.4 %shard_map.100 = (bf16[384,2048]{1,0:T(8,128)(2,1)}, f32[384,704]{1,0:T(8,128)}, f32[384,704]{1,0:T(8,128)}) custom-call(s32[17]{0:T(128)} %stack.116.pos_ref, f32[1,2048]{1,0:T(1,128)} %bitcast.59, bf16[384,512]{1,0:T(8,128)(2,1)} %refs_0_.3, bf16[384,512]{1,0:T(8,128)(2,1)} %copy-done.6, bf16[384,512]{1,0:T(8,128)(2,1)} %copy-done.7, ...), custom_call_target="tpu_custom_call" | custom-call | tf_op jit(solution)/shard_map/pallas_call | solution.py:225
  190.2 6.8 %shard_map.101 = (f32[384,512]{1,0:T(8,128)}, bf16[384,512]{1,0:T(8,128)(2,1)}, bf16[384,512]{1,0:T(8,128)(2,1)}, bf16[384,512]{1,0:T(8,128)(2,1)}) custom-call(s32[16]{0:T(128)} %stack.115.pos_ref, bf16[384,2048]{1,0:T(8,128)(2,1)} %get-tuple-element.12.x_ref, f32[384,704]{1,0:T(8,128)} %get-tuple-element.13.gate_in, f32[384,704]{1,0:T(8,128)} %get-tuple-element.14.up_in, ...), custom_call_target="tpu_custom_call" | custom-call | tf_op jit(solution)/shard_map/pallas_call | solution.py:261
  197.0 2.5 %collective-permute-start.24 = (bf16[384,512]{1,0:T(8,128)(2,1)}, bf16[384,512]{1,0:T(8,128)(2,1)S(1)}, u32[]{:S(2)}, u32[]{:S(2)}) collective-permute-start(bf16[384,512]{1,0:T(8,128)(2,1)} %get-tuple-element.16), channel_id=1, source_target_pairs={{0,8},{8,0},{16,24},{24,16},{1,9},{9,1},{17,25},{25,17},{2,10},{10... | collective-permute-start | bytes 1179656 | tf_op jit(solution)/shard_map/ppermute | solution.py:22
  200.8 5.5 %collective-permute-start.26 = (bf16[384,512]{1,0:T(8,128)(2,1)}, bf16[384,512]{1,0:T(8,128)(2,1)S(1)}, u32[]{:S(2)}, u32[]{:S(2)}) collective-permute-start(bf16[384,512]{1,0:T(8,128)(2,1)} %get-tuple-element.17), channel_id=1, source_target_pairs={{16,0},{8,24},{17,1},{9,25},{18,2},{10,26},{19,3},{11,27},{20,4},{... | collective-permute-start | bytes 1179656 | tf_op jit(solution)/shard_map/ppermute | solution.py:44
  206.3 3.6 %collective-permute-start.27 = (bf16[384,512]{1,0:T(8,128)(2,1)}, bf16[384,512]{1,0:T(8,128)(2,1)S(1)}, u32[]{:S(2)}, u32[]{:S(2)}) collective-permute-start(bf16[384,512]{1,0:T(8,128)(2,1)} %get-tuple-element.18), channel_id=1, source_target_pairs={{8,16},{16,8},{9,17},{17,9},{10,18},{18,10},{11,19},{19,11},{12,20... | collective-permute-start | bytes 1179656 | tf_op jit(solution)/shard_map/ppermute | solution.py:41
  211.9 7.4 %collective-permute-done.25.refs_1_ = bf16[384,512]{1,0:T(8,128)(2,1)S(1)} collective-permute-done((bf16[384,512]{1,0:T(8,128)(2,1)}, bf16[384,512]{1,0:T(8,128)(2,1)S(1)}, u32[]{:S(2)}, u32[]{:S(2)}) %collective-permute-start.25) | collective-permute-done | bytes 393248 | tf_op jit(solution)/shard_map/ppermute | solution.py:42
  219.3 13.5 %collective-permute-done.26.refs_2_ = bf16[384,512]{1,0:T(8,128)(2,1)S(1)} collective-permute-done((bf16[384,512]{1,0:T(8,128)(2,1)}, bf16[384,512]{1,0:T(8,128)(2,1)S(1)}, u32[]{:S(2)}, u32[]{:S(2)}) %collective-permute-start.26) | collective-permute-done | bytes 393248 | tf_op jit(solution)/shard_map/ppermute | solution.py:44
  232.9 9.1 %collective-permute-done.27.refs_3_ = bf16[384,512]{1,0:T(8,128)(2,1)S(1)} collective-permute-done((bf16[384,512]{1,0:T(8,128)(2,1)}, bf16[384,512]{1,0:T(8,128)(2,1)S(1)}, u32[]{:S(2)}, u32[]{:S(2)}) %collective-permute-start.27) | collective-permute-done | bytes 393248 | tf_op jit(solution)/shard_map/ppermute | solution.py:41
  243.1 3.8 %shard_map.107 = bf16[384,512]{1,0:T(8,128)(2,1)} custom-call(s32[1]{0:T(128)} %bitcast.pos_ref, f32[384,512]{1,0:T(8,128)} %get-tuple-element.15.own_ref, bf16[384,512]{1,0:T(8,128)(2,1)} %copy-done.14, bf16[384,512]{1,0:T(8,128)(2,1)} %copy-done.15, bf16[384,512]{1,0:T(8,128)(2,1)} %copy-done.16, bf16[384,512]{1,0:T(8,128)(2,1)} %copy-done.17, ...), custom_call_target="tpu_custom_call" | custom-call | tf_op jit(solution)/shard_map/pallas_call | solution.py:293
  (134 shorter events, 37.0 us)
Async XLA Ops:
  15.9 46.7 %all-to-all-start.1 = ((bf16[8,96,1024]{2,1,0:T(8,128)(2,1)}), bf16[8,96,1024]{2,1,0:T(8,128)(2,1)S(1)}, u32[]{:S(2)}, u32[]{:S(2)}) async-start(bf16[8,96,1024]{2,1,0:T(8,128)(2,1)} %bitcast.42), calls=%async_computation.1 | async-start | bytes 3145728 | tf_op jit(solution)/shard_map/all_to_all | solution.py:376
  21.0 28.9 %collective-permute-start.1 = (bf16[384,512]{1,0:T(8,128)(2,1)S(1)}, bf16[384,512]{1,0:T(8,128)(2,1)S(1)}, u32[]{:S(2)}, u32[]{:S(2)}) collective-permute-start(bf16[384,512]{1,0:T(8,128)(2,1)S(1)} %copy-done.5), channel_id=1, source_target_pairs={{0,16},{8,24},{16,0},{24,8},{1,17},{9,25},{17,1},{25,9},{2,18},{10... | collective-permute-start | bytes 1179656 | tf_op jit(solution)/shard_map/ppermute | solution.py:22
  23.5 34.7 %collective-permute-start.2 = (bf16[384,512]{1,0:T(8,128)(2,1)S(1)}, bf16[384,512]{1,0:T(8,128)(2,1)S(1)}, u32[]{:S(2)}, u32[]{:S(2)}) collective-permute-start(bf16[384,512]{1,0:T(8,128)(2,1)S(1)} %copy-done.5), channel_id=1, source_target_pairs={{0,24},{8,16},{16,8},{24,0},{1,25},{9,17},{17,9},{25,1},{2,26},{10... | collective-permute-start | bytes 1179656 | tf_op jit(solution)/shard_map/ppermute | solution.py:22
  63.7 41.8 %all-to-all-start.2 = ((bf16[8,96,1024]{2,1,0:T(8,128)(2,1)}), bf16[8,96,1024]{2,1,0:T(8,128)(2,1)S(1)}, u32[]{:S(2)}, u32[]{:S(2)}) async-start(bf16[8,96,1024]{2,1,0:T(8,128)(2,1)} %bitcast.40), calls=%async_computation.2 | async-start | bytes 3145728 | tf_op jit(solution)/shard_map/all_to_all | solution.py:376
  67.9 26.5 %collective-permute-start.3 = (bf16[704,256]{1,0:T(8,128)(2,1)}, bf16[704,256]{1,0:T(8,128)(2,1)}, u32[]{:S(2)}, u32[]{:S(2)}) collective-permute-start(bf16[704,256]{1,0:T(8,128)(2,1)} %bitcast.49), channel_id=1, source_target_pairs={{0,2},{1,3},{2,0},{3,1},{4,6},{5,7},{6,4},{7,5},{8,10},{9,11},{10,... | collective-permute-start | bytes 1081352 | tf_op jit(solution)/shard_map/ppermute | solution.py:22
  67.9 27.3 %collective-permute-start.4 = (bf16[704,256]{1,0:T(8,128)(2,1)}, bf16[704,256]{1,0:T(8,128)(2,1)}, u32[]{:S(2)}, u32[]{:S(2)}) collective-permute-start(bf16[704,256]{1,0:T(8,128)(2,1)} %bitcast.50), channel_id=1, source_target_pairs={{0,4},{1,5},{2,6},{3,7},{4,0},{5,1},{6,2},{7,3},{8,12},{9,13},{10,... | collective-permute-start | bytes 1081352 | tf_op jit(solution)/shard_map/ppermute | solution.py:22
  69.9 27.4 %collective-permute-start.5 = (bf16[704,256]{1,0:T(8,128)(2,1)}, bf16[704,256]{1,0:T(8,128)(2,1)}, u32[]{:S(2)}, u32[]{:S(2)}) collective-permute-start(bf16[704,256]{1,0:T(8,128)(2,1)} %bitcast.51), channel_id=1, source_target_pairs={{0,1},{1,0},{2,3},{3,2},{4,5},{5,4},{6,7},{7,6},{8,9},{9,8},{10,11... | collective-permute-start | bytes 1081352 | tf_op jit(solution)/shard_map/ppermute | solution.py:22
  69.9 32.2 %collective-permute-start.8 = (bf16[704,256]{1,0:T(8,128)(2,1)}, bf16[704,256]{1,0:T(8,128)(2,1)}, u32[]{:S(2)}, u32[]{:S(2)}) collective-permute-start(bf16[704,256]{1,0:T(8,128)(2,1)} %bitcast.53), channel_id=1, source_target_pairs={{0,2},{1,3},{2,0},{3,1},{4,6},{5,7},{6,4},{7,5},{8,10},{9,11},{10,... | collective-permute-start | bytes 1081352 | tf_op jit(solution)/shard_map/ppermute | solution.py:22
  71.4 43.4 %collective-permute-start.9 = (bf16[704,256]{1,0:T(8,128)(2,1)}, bf16[704,256]{1,0:T(8,128)(2,1)}, u32[]{:S(2)}, u32[]{:S(2)}) collective-permute-start(bf16[704,256]{1,0:T(8,128)(2,1)} %bitcast.54), channel_id=1, source_target_pairs={{0,4},{1,5},{2,6},{3,7},{4,0},{5,1},{6,2},{7,3},{8,12},{9,13},{10,... | collective-permute-start | bytes 1081352 | tf_op jit(solution)/shard_map/ppermute | solution.py:22
  94.4 20.5 %collective-permute-start.10 = (bf16[704,256]{1,0:T(8,128)(2,1)}, bf16[704,256]{1,0:T(8,128)(2,1)}, u32[]{:S(2)}, u32[]{:S(2)}) collective-permute-start(bf16[704,256]{1,0:T(8,128)(2,1)} %bitcast.55), channel_id=1, source_target_pairs={{0,1},{1,0},{2,3},{3,2},{4,5},{5,4},{6,7},{7,6},{8,9},{9,8},{10,11... | collective-permute-start | bytes 1081352 | tf_op jit(solution)/shard_map/ppermute | solution.py:22
  95.3 19.7 %collective-permute-start.15 = (bf16[704,256]{1,0:T(8,128)(2,1)}, bf16[704,256]{1,0:T(8,128)(2,1)S(1)}, u32[]{:S(2)}, u32[]{:S(2)}) collective-permute-start(bf16[704,256]{1,0:T(8,128)(2,1)} %bitcast.56), channel_id=1, source_target_pairs={{0,6},{1,7},{2,4},{3,5},{4,2},{5,3},{6,0},{7,1},{8,14},{9,15},{10,... | collective-permute-start | bytes 1081352 | tf_op jit(solution)/shard_map/ppermute | solution.py:22
  97.4 20.0 %collective-permute-start.17 = (bf16[704,256]{1,0:T(8,128)(2,1)S(1)}, bf16[704,256]{1,0:T(8,128)(2,1)S(1)}, u32[]{:S(2)}, u32[]{:S(2)}) collective-permute-start(bf16[704,256]{1,0:T(8,128)(2,1)S(1)} %copy-done.19), channel_id=1, source_target_pairs={{0,2},{1,3},{2,0},{3,1},{4,6},{5,7},{6,4},{7,5},{8,10},{9,11},{10,... | collective-permute-start | bytes 1081352 | tf_op jit(solution)/shard_map/ppermute | solution.py:22
  102.1 16.2 %collective-permute-start.18 = (bf16[704,256]{1,0:T(8,128)(2,1)S(1)}, bf16[704,256]{1,0:T(8,128)(2,1)S(1)}, u32[]{:S(2)}, u32[]{:S(2)}) collective-permute-start(bf16[704,256]{1,0:T(8,128)(2,1)S(1)} %copy-done.19), channel_id=1, source_target_pairs={{0,4},{1,5},{2,6},{3,7},{4,0},{5,1},{6,2},{7,3},{8,12},{9,13},{10,... | collective-permute-start | bytes 1081352 | tf_op jit(solution)/shard_map/ppermute | solution.py:22
  115.0 24.8 %collective-permute-start.6 = (bf16[704,256]{1,0:T(8,128)(2,1)}, bf16[704,256]{1,0:T(8,128)(2,1)}, u32[]{:S(2)}, u32[]{:S(2)}) collective-permute-start(bf16[704,256]{1,0:T(8,128)(2,1)} %collective-permute-done.3.refs_5_), channel_id=1, source_target_pairs={{0,1},{1,0},{2,3},{3,2},{4,5},{5,4},{6,7},{7,6},{8,9},{9,8},{10,11... | collective-permute-start | bytes 1081352 | tf_op jit(solution)/shard_map/ppermute | solution.py:22
  117.4 23.7 %collective-permute-start.7 = (bf16[704,256]{1,0:T(8,128)(2,1)}, bf16[704,256]{1,0:T(8,128)(2,1)}, u32[]{:S(2)}, u32[]{:S(2)}) collective-permute-start(bf16[704,256]{1,0:T(8,128)(2,1)} %collective-permute-done.4.refs_6_), channel_id=1, source_target_pairs={{0,1},{1,0},{2,3},{3,2},{4,5},{5,4},{6,7},{7,6},{8,9},{9,8},{10,11... | collective-permute-start | bytes 1081352 | tf_op jit(solution)/shard_map/ppermute | solution.py:22
  118.4 23.4 %collective-permute-start.31 = (bf16[704,384]{1,0:T(8,128)(2,1)}, bf16[704,384]{1,0:T(8,128)(2,1)S(1)}, u32[]{:S(2)}, u32[]{:S(2)}) collective-permute-start(bf16[704,384]{1,0:T(8,128)(2,1)} %shard_map.104.refs_0_), channel_id=1, source_target_pairs={{8,16},{16,8},{9,17},{17,9},{10,18},{18,10},{11,19},{19,11},{12,20... | collective-permute-start | bytes 1622024 | tf_op jit(solution)/shard_map/ppermute | solution.py:27
  125.6 24.6 %collective-permute-start.11 = (bf16[704,256]{1,0:T(8,128)(2,1)}, bf16[704,256]{1,0:T(8,128)(2,1)}, u32[]{:S(2)}, u32[]{:S(2)}) collective-permute-start(bf16[704,256]{1,0:T(8,128)(2,1)} %collective-permute-done.8.refs_11_), channel_id=1, source_target_pairs={{0,1},{1,0},{2,3},{3,2},{4,5},{5,4},{6,7},{7,6},{8,9},{9,8},{10,11... | collective-permute-start | bytes 1081352 | tf_op jit(solution)/shard_map/ppermute | solution.py:22
  128.0 22.4 %collective-permute-start.12 = (bf16[704,256]{1,0:T(8,128)(2,1)}, bf16[704,256]{1,0:T(8,128)(2,1)}, u32[]{:S(2)}, u32[]{:S(2)}) collective-permute-start(bf16[704,256]{1,0:T(8,128)(2,1)} %collective-permute-done.9.refs_12_), channel_id=1, source_target_pairs={{0,1},{1,0},{2,3},{3,2},{4,5},{5,4},{6,7},{7,6},{8,9},{9,8},{10,11... | collective-permute-start | bytes 1081352 | tf_op jit(solution)/shard_map/ppermute | solution.py:22
  134.7 43.4 %all-to-all-start.3 = ((bf16[8,96,512]{2,1,0:T(8,128)(2,1)}), bf16[8,96,512]{2,1,0:T(8,128)(2,1)S(1)}, u32[]{:S(2)}, u32[]{:S(2)}) async-start(bf16[8,96,512]{2,1,0:T(8,128)(2,1)} %bitcast.46), calls=%async_computation.3 | async-start | bytes 1572864 | tf_op jit(solution)/shard_map/all_to_all | solution.py:440
  139.8 20.9 %collective-permute-start.30 = (bf16[704,384]{1,0:T(8,128)(2,1)S(1)}, bf16[704,384]{1,0:T(8,128)(2,1)S(1)}, u32[]{:S(2)}, u32[]{:S(2)}) collective-permute-start(bf16[704,384]{1,0:T(8,128)(2,1)S(1)} %copy-done.4), channel_id=1, source_target_pairs={{0,16},{24,8},{1,17},{25,9},{2,18},{26,10},{3,19},{27,11},{4,20},{... | collective-permute-start | bytes 1622024 | tf_op jit(solution)/shard_map/ppermute | solution.py:28
  141.1 19.8 %collective-permute-start.33 = (bf16[704,384]{1,0:T(8,128)(2,1)S(1)}, bf16[704,384]{1,0:T(8,128)(2,1)S(1)}, u32[]{:S(2)}, u32[]{:S(2)}) collective-permute-start(bf16[704,384]{1,0:T(8,128)(2,1)S(1)} %copy-done.4), channel_id=1, source_target_pairs={{0,24},{24,0},{1,25},{25,1},{2,26},{26,2},{3,27},{27,3},{4,28},{28... | collective-permute-start | bytes 1622024 | tf_op jit(solution)/shard_map/ppermute | solution.py:30
  141.8 31.0 %collective-permute-start.32 = (bf16[704,384]{1,0:T(8,128)(2,1)S(1)}, bf16[704,384]{1,0:T(8,128)(2,1)S(1)}, u32[]{:S(2)}, u32[]{:S(2)}) collective-permute-start(bf16[704,384]{1,0:T(8,128)(2,1)S(1)} %collective-permute-done.31.refs_2_), channel_id=1, source_target_pairs={{16,24},{8,0},{17,25},{9,1},{18,26},{10,2},{19,27},{11,3},{20,28},... | collective-permute-start | bytes 1622024 | tf_op jit(solution)/shard_map/ppermute | solution.py:29
  160.2 29.9 %collective-permute-start.20 = (bf16[704,256]{1,0:T(8,128)(2,1)}, bf16[704,256]{1,0:T(8,128)(2,1)}, u32[]{:S(2)}, u32[]{:S(2)}) collective-permute-start(bf16[704,256]{1,0:T(8,128)(2,1)} %copy-done.21), channel_id=1, source_target_pairs={{0,1},{1,0},{2,3},{3,2},{4,5},{5,4},{6,7},{7,6},{8,9},{9,8},{10,11... | collective-permute-start | bytes 1081352 | tf_op jit(solution)/shard_map/ppermute | solution.py:22
  160.3 29.8 %collective-permute-start.16 = (bf16[704,256]{1,0:T(8,128)(2,1)}, bf16[704,256]{1,0:T(8,128)(2,1)}, u32[]{:S(2)}, u32[]{:S(2)}) collective-permute-start(bf16[704,256]{1,0:T(8,128)(2,1)} %copy-done.20), channel_id=1, source_target_pairs={{0,1},{1,0},{2,3},{3,2},{4,5},{5,4},{6,7},{7,6},{8,9},{9,8},{10,11... | collective-permute-start | bytes 1081352 | tf_op jit(solution)/shard_map/ppermute | solution.py:22
  160.7 29.4 %collective-permute-start.21 = (bf16[704,256]{1,0:T(8,128)(2,1)}, bf16[704,256]{1,0:T(8,128)(2,1)}, u32[]{:S(2)}, u32[]{:S(2)}) collective-permute-start(bf16[704,256]{1,0:T(8,128)(2,1)} %copy-done.22), channel_id=1, source_target_pairs={{0,1},{1,0},{2,3},{3,2},{4,5},{5,4},{6,7},{7,6},{8,9},{9,8},{10,11... | collective-permute-start | bytes 1081352 | tf_op jit(solution)/shard_map/ppermute | solution.py:22
  160.9 29.3 %collective-permute-start.14 = (bf16[704,256]{1,0:T(8,128)(2,1)}, bf16[704,256]{1,0:T(8,128)(2,1)}, u32[]{:S(2)}, u32[]{:S(2)}) collective-permute-start(bf16[704,256]{1,0:T(8,128)(2,1)} %collective-permute-done.13.refs_0_), channel_id=1, source_target_pairs={{0,1},{1,0},{2,3},{3,2},{4,5},{5,4},{6,7},{7,6},{8,9},{9,8},{10,11... | collective-permute-start | bytes 1081352 | tf_op jit(solution)/shard_map/ppermute | solution.py:22
  172.8 17.3 %collective-permute-start.23 = (bf16[704,256]{1,0:T(8,128)(2,1)}, bf16[704,256]{1,0:T(8,128)(2,1)}, u32[]{:S(2)}, u32[]{:S(2)}) collective-permute-start(bf16[704,256]{1,0:T(8,128)(2,1)} %collective-permute-done.22.refs_10_), channel_id=1, source_target_pairs={{0,1},{1,0},{2,3},{3,2},{4,5},{5,4},{6,7},{7,6},{8,9},{9,8},{10,11... | collective-permute-start | bytes 1081352 | tf_op jit(solution)/shard_map/ppermute | solution.py:22
  178.2 63.8 %all-to-all-start.4 = ((bf16[8,96,512]{2,1,0:T(8,128)(2,1)}), bf16[8,96,512]{2,1,0:T(8,128)(2,1)S(1)}, u32[]{:S(2)}, u32[]{:S(2)}) async-start(bf16[8,96,512]{2,1,0:T(8,128)(2,1)} %bitcast.43), calls=%async_computation.4 | async-start | bytes 1572864 | tf_op jit(solution)/shard_map/all_to_all | solution.py:440
  199.5 19.8 %collective-permute-start.25 = (bf16[384,512]{1,0:T(8,128)(2,1)}, bf16[384,512]{1,0:T(8,128)(2,1)S(1)}, u32[]{:S(2)}, u32[]{:S(2)}) collective-permute-start(bf16[384,512]{1,0:T(8,128)(2,1)} %get-tuple-element.17), channel_id=1, source_target_pairs={{0,16},{24,8},{1,17},{25,9},{2,18},{26,10},{3,19},{27,11},{4,20},{... | collective-permute-start | bytes 1179656 | tf_op jit(solution)/shard_map/ppermute | solution.py:42
  200.8 32.1 %collective-permute-start.26 = (bf16[384,512]{1,0:T(8,128)(2,1)}, bf16[384,512]{1,0:T(8,128)(2,1)S(1)}, u32[]{:S(2)}, u32[]{:S(2)}) collective-permute-start(bf16[384,512]{1,0:T(8,128)(2,1)} %get-tuple-element.17), channel_id=1, source_target_pairs={{16,0},{8,24},{17,1},{9,25},{18,2},{10,26},{19,3},{11,27},{20,4},{... | collective-permute-start | bytes 1179656 | tf_op jit(solution)/shard_map/ppermute | solution.py:44
  206.3 35.7 %collective-permute-start.27 = (bf16[384,512]{1,0:T(8,128)(2,1)}, bf16[384,512]{1,0:T(8,128)(2,1)S(1)}, u32[]{:S(2)}, u32[]{:S(2)}) collective-permute-start(bf16[384,512]{1,0:T(8,128)(2,1)} %get-tuple-element.18), channel_id=1, source_target_pairs={{8,16},{16,8},{9,17},{17,9},{10,18},{18,10},{11,19},{19,11},{12,20... | collective-permute-start | bytes 1179656 | tf_op jit(solution)/shard_map/ppermute | solution.py:41
  209.9 32.1 %collective-permute-start.28 = (bf16[384,512]{1,0:T(8,128)(2,1)}, bf16[384,512]{1,0:T(8,128)(2,1)S(1)}, u32[]{:S(2)}, u32[]{:S(2)}) collective-permute-start(bf16[384,512]{1,0:T(8,128)(2,1)} %get-tuple-element.18), channel_id=1, source_target_pairs={{0,24},{24,0},{1,25},{25,1},{2,26},{26,2},{3,27},{27,3},{4,28},{28... | collective-permute-start | bytes 1179656 | tf_op jit(solution)/shard_map/ppermute | solution.py:45
  (32 other events, 318.9 us)

commit v2 on v1

v2 whole, which is shorter than its diff:
```python
import jax
import jax.numpy as jnp
from jax import lax
from jax.experimental import pallas as pl
from jax.experimental.pallas import tpu as pltpu
from jax.sharding import PartitionSpec as P


norm_eps = 1e-06
F32 = jnp.float32
BF16 = jnp.bfloat16
MIB = 1 << 20


VMEM_SPEC = pl.BlockSpec(memory_space=pltpu.VMEM)
SMEM_SPEC = pl.BlockSpec(memory_space=pltpu.SMEM)
HBM_SPEC = pl.BlockSpec(memory_space=pltpu.HBM)


def swap(x, axis, mask):
    count = lax.axis_size(axis)
    return lax.ppermute(x, axis, [(i, i ^ mask) for i in range(count)])


def direct_gather(near, far, axis):
    pieces = [([near], 0)]
    for mask, x in ((1, near), (2, far), (3, far)):
        pieces.append(([swap(x, axis, mask)], mask))
    return pieces


def box_gather(x, axis, relay):
    near = {2: swap(x, axis, 2), 4: swap(x, axis, 4)}
    diagonal = swap(near.get(6 - relay, x), axis, relay)
    pieces = [(x, 0), (near[2], 2), (near[4], 4)]
    pieces += [(swap(a, axis, 1), m ^ 1) for a, m in pieces]
    pieces += [(diagonal, 6), (swap(diagonal, axis, 1), 7)]
    return [([a], m) for a, m in pieces]


def arrays_of(pieces):
    return [a for arrays, _ in pieces for a in arrays]


def read_piece(arrays, refs, at, flag):
    if len(arrays) == 1:
        return refs[at][...]
    return jnp.where(flag != 0, refs[at][...], refs[at + 1][...])


def copy_pieces(pieces, refs, flag, pos_ref, slot, target, dim):
    at = 0
    for number, (arrays, _) in enumerate(pieces):
        value = read_piece(arrays, refs, at, flag)
        at += len(arrays)
        if len(pieces) == 1:
            target[...] = value
        elif dim == 0:
            row = pl.multiple_of(pos_ref[slot + number], 64)
            target[pl.ds(row, value.shape[0]), :] = value
        else:
            col = pl.multiple_of(pos_ref[slot + number], 128)
            target[:, pl.ds(col, value.shape[1])] = value


def stack_scalars(values):
    return jnp.stack([jnp.asarray(v, jnp.int32) for v in values])


def silu(v):
    return v / (1.0 + jnp.exp(-v))


def normalise(x_ref, gain_ref):
    wide = x_ref[...].astype(F32)
    scale = lax.rsqrt(jnp.mean(wide * wide, axis=1, keepdims=True) + norm_eps)
    x_ref[...] = (wide * scale * gain_ref[...]).astype(BF16)


def dot(a, b, dims):
    return lax.dot_general(a, b, (dims, ((), ())), preferred_element_type=F32)


def one_hot(ids, shape, dim):
    span = lax.broadcasted_iota(jnp.int32, shape, dim)
    return jnp.where(ids == span, 1.0, 0.0).astype(BF16)


def as_column(row):
    return jnp.transpose(jnp.broadcast_to(row, (8, row.shape[1])))[:, :1]


def kernel(body, out_shape, in_specs, scratch_shapes, mib):
    outs = len(out_shape) if isinstance(out_shape, list) else None
    return pl.pallas_call(
        body,
        out_shape=out_shape,
        in_specs=in_specs,
        out_specs=VMEM_SPEC if outs is None else [VMEM_SPEC] * outs,
        scratch_shapes=scratch_shapes,
        compiler_params=pltpu.CompilerParams(vmem_limit_bytes=mib * MIB),
    )


def take_windows(pieces, flag, ids_lanes):
    arrays = arrays_of(pieces)
    tok_dev, width = arrays[0].shape
    slots = ids_lanes.shape[1]

    def body(pos_ref, ids_ref, *refs):
        picker = one_hot(as_column(ids_ref[...]), (slots, tok_dev), 1)
        at = 0
        for number, (alternatives, _) in enumerate(pieces):
            value = read_piece(alternatives, refs, at, pos_ref[0])
            at += len(alternatives)
            rows = dot(picker, value, ((1,), (0,))).astype(BF16)
            refs[-1][:, number * width : (number + 1) * width] = rows

    return kernel(
        body,
        jax.ShapeDtypeStruct((slots, width * len(pieces)), BF16),
        [SMEM_SPEC] + [VMEM_SPEC] * (1 + len(arrays)),
        [],
        60,
    )(flag, ids_lanes, *arrays)


def as_row(column):
    return jnp.transpose(jnp.broadcast_to(column, (column.shape[0], 128)))[:1, :]


def expert_hidden(window, width, positions, slot_lanes, gain, gate, up, cap, begun, last):
    hidden, features = gate.shape
    parts = window.shape[1] // width
    prior = 3 if begun else 0

    def body(pos_ref, slot_ref, gain_ref, gate_hbm, up_hbm, window_ref, *refs):
        outs = refs[prior:-4]
        gate_ref, up_ref, x_ref, sems = refs[-4:]
        cols = [pl.multiple_of(pos_ref[n], 128) for n in range(parts)]
        copies = []
        for matrix, (source, target) in enumerate(((gate_hbm, gate_ref), (up_hbm, up_ref))):
            for n, col in enumerate(cols):
                copy = pltpu.make_async_copy(
                    source.at[:, pl.ds(col, width)],
                    target.at[:, pl.ds(n * width, width)],
                    sems.at[matrix * parts + n],
                )
                copy.start()
                copies.append(copy)
        picker = one_hot(slot_ref[...], (cap, slot_ref.shape[1]), 0)
        rows = dot(picker, window_ref[...], ((1,), (0,)))
        squares = as_row(jnp.sum(rows * rows, axis=1, keepdims=True))
        for n, col in enumerate(cols):
            span = slice(n * width, (n + 1) * width)
            x_ref[:, span] = (rows[:, span] * gain_ref[:, pl.ds(col, width)]).astype(BF16)
        for copy in copies[:parts]:
            copy.wait()
        gates = dot(gate_ref[...], x_ref[...], ((1,), (1,)))
        for copy in copies[parts:]:
            copy.wait()
        ups = dot(up_ref[...], x_ref[...], ((1,), (1,)))
        if begun:
            gates = gates + refs[0][...]
            ups = ups + refs[1][...]
            squares = squares + refs[2][...]
        if last:
            scale = lax.rsqrt(squares * (1.0 / features) + norm_eps)
            outs[0][...] = (silu(gates * scale) * (ups * scale)).astype(BF16)
        else:
            outs[0][...] = gates
            outs[1][...] = ups
            outs[2][...] = squares

    products = jax.ShapeDtypeStruct((hidden, cap), F32)
    result = [jax.ShapeDtypeStruct((hidden, cap), BF16)]
    if not last:
        result = [products, products, jax.ShapeDtypeStruct((1, cap), F32)]
    return kernel(
        body,
        result,
        [SMEM_SPEC, VMEM_SPEC, VMEM_SPEC] + [HBM_SPEC] * 2 + [VMEM_SPEC] * (1 + prior),
        [
            pltpu.VMEM((hidden, parts * width), BF16),
            pltpu.VMEM((hidden, parts * width), BF16),
            pltpu.VMEM((cap, parts * width), BF16),
            pltpu.SemaphoreType.DMA((2 * parts,)),
        ],
        56,
    )(positions, slot_lanes, gain, gate, up, window, *(begun or []))


def expert_down(hidden_pieces, positions, downs, gate_lanes, slot_lanes):
    _, hidden, width = downs.shape
    cap = gate_lanes.shape[1]
    slots = slot_lanes.shape[1]
    arrays = arrays_of(hidden_pieces)

    def body(pos_ref, gate_ref, slot_ref, down_hbm, *refs):
        out_ref, hidden_ref, down_ref, sem = refs[len(arrays) :]
        expert = pos_ref[1 + len(hidden_pieces)]
        copy = pltpu.make_async_copy(down_hbm.at[expert], down_ref, sem)
        copy.start()
        copy_pieces(hidden_pieces, refs, pos_ref[0], pos_ref, 1, hidden_ref, 0)
        picker = one_hot(as_column(slot_ref[...]), (slots, cap), 1)
        gate = as_column(gate_ref[...])
        copy.wait()
        out = dot(hidden_ref[...], down_ref[...], ((0,), (0,)))
        weighted = (gate * out).astype(BF16)
        out_ref[...] = dot(picker, weighted, ((1,), (0,))).astype(BF16)

    return kernel(
        body,
        jax.ShapeDtypeStruct((slots, width), BF16),
        [SMEM_SPEC, VMEM_SPEC, VMEM_SPEC, HBM_SPEC] + [VMEM_SPEC] * len(arrays),
        [
            pltpu.VMEM((hidden, cap), BF16),
            pltpu.VMEM((hidden, width), BF16),
            pltpu.SemaphoreType.DMA(()),
        ],
        60,
    )(positions, gate_lanes, slot_lanes, downs, *arrays)


def add_products(x_ref, total_ref, weights, positions, first):
    for number, (weight, col) in enumerate(zip(weights, positions)):
        x = x_ref[:, pl.ds(pl.multiple_of(col, 128), weight.shape[1])]
        part = dot(x, weight[...], ((1,), (1,)))
        if first and number == 0:
            total_ref[...] = part
        else:
            total_ref[...] += part


def shared_in(token_pieces, gates, ups, positions, gain):
    token_arrays = arrays_of(token_pieces)
    gate_arrays, up_arrays = arrays_of(gates), arrays_of(ups)
    tok_dev = token_arrays[0].shape[0]
    features = gain.shape[1]
    hidden = gate_arrays[0].shape[0]
    ends = [len(token_arrays), len(token_arrays) + len(gate_arrays)]
    count = ends[1] + len(up_arrays)

    def body(pos_ref, gain_ref, *refs):
        x_ref, gate_sum, up_sum = refs[count:]
        copy_pieces(token_pieces, refs, pos_ref[0], pos_ref, 1, x_ref, 1)
        normalise(x_ref, gain_ref)
        first = 1 + len(token_pieces)
        at = [pos_ref[first + n] for n in range(len(gate_arrays) + len(up_arrays))]
        add_products(x_ref, gate_sum, refs[ends[0] : ends[1]], at[: len(gate_arrays)], True)
        add_products(x_ref, up_sum, refs[ends[1] : count], at[len(gate_arrays) :], True)

    return kernel(
        body,
        [
            jax.ShapeDtypeStruct((tok_dev, features), BF16),
            jax.ShapeDtypeStruct((tok_dev, hidden), F32),
            jax.ShapeDtypeStruct((tok_dev, hidden), F32),
        ],
        [SMEM_SPEC] + [VMEM_SPEC] * (1 + count),
        [],
        60,
    )(positions, gain, *token_arrays, *gate_arrays, *up_arrays)


def shared_out(begun, gates, ups, downs, positions, width, blocks):
    arrays = arrays_of(gates) + arrays_of(ups) + arrays_of(downs)
    ends = [len(gates), len(gates) + len(ups)]
    count = len(arrays)
    tok_dev, features = begun[0].shape
    hidden = begun[1].shape[1]
    block = arrays[-1].shape[1]

    def body(pos_ref, x_ref, gate_in, up_in, *refs):
        outs = refs[count:-3]
        gate_sum, up_sum, sum_ref = refs[-3:]
        at = [pos_ref[n] for n in range(count)]
        gate_sum[...] = gate_in[...]
        add_products(x_ref, gate_sum, refs[: ends[0]], at[: ends[0]], False)
        up_sum[...] = up_in[...]
        add_products(x_ref, up_sum, refs[ends[0] : ends[1]], at[ends[0] : ends[1]], False)
        mid = (silu(gate_sum[...]) * up_sum[...]).astype(BF16)
        for number in range(ends[1], count):
            col = pl.multiple_of(at[number], 128)
            sum_ref[:, pl.ds(col, block)] = dot(mid, refs[number][...], ((1,), (0,)))
        for number in range(blocks):
            col = pl.multiple_of(pos_ref[count + number], 128)
            block_sum = sum_ref[:, pl.ds(col, width)]
            if number < 2:
                outs[number][...] = block_sum
            else:
                rows = slice((number - 2) * tok_dev, (number - 1) * tok_dev)
                outs[2][rows, :] = block_sum.astype(BF16)

    return kernel(
        body,
        [jax.ShapeDtypeStruct((tok_dev, width), F32)] * min(blocks, 2)
        + [jax.ShapeDtypeStruct(((blocks - 2) * tok_dev, width), BF16)] * (blocks > 2),
        [SMEM_SPEC] + [VMEM_SPEC] * (3 + count),
        [
            pltpu.VMEM((tok_dev, hidden), F32),
            pltpu.VMEM((tok_dev, hidden), F32),
            pltpu.VMEM((tok_dev, features), F32),
        ],
        60,
    )(positions, *begun, *arrays)


def finish(shared_own, shared_parts, windows, ids, tok_dev):
    width = shared_own.shape[1]
    parts = len(shared_parts)

    def body(own_ref, *refs):
        total = own_ref[...]
        for number in range(parts):
            total = total + refs[number][:tok_dev, :].astype(F32)
        for number in range(len(windows)):
            values, id_ref = refs[parts + number], refs[parts + len(windows) + number]
            picker = one_hot(id_ref[...], (tok_dev, values.shape[0]), 0)
            total = total + dot(picker, values[...], ((1,), (0,)))
        refs[-1][...] = total.astype(BF16)

    return kernel(
        body,
        jax.ShapeDtypeStruct((tok_dev, width), BF16),
        [VMEM_SPEC] * (1 + parts + 2 * len(windows)),
        [],
        54,
    )(shared_own, *shared_parts, *windows, *ids)


def on_device(
    tokens,
    norm_gain,
    shared_gate,
    shared_up,
    shared_down,
    expert_gate,
    expert_up,
    expert_down_weight,
    chosen,
    gates,
):
    tp_count = lax.axis_size("tp")
    ep_count = lax.axis_size("ep")
    tp = lax.axis_index("tp").astype(jnp.int32)
    ep = lax.axis_index("ep").astype(jnp.int32)
    tok_dev, width = tokens.shape
    experts, cap = chosen.shape
    split = tp_count // experts
    on_line = tp_count == 4 and experts == 2
    on_box = ep_count == 8
    inner = ((tp == 1) | (tp == 2)).astype(jnp.int32)
    gain = norm_gain[None, :]
    gate_weight = expert_gate.reshape(expert_gate.shape[2], expert_gate.shape[3])
    up_weight = expert_up.reshape(expert_up.shape[2], expert_up.shape[3])

    own_expert = tp // split
    order = [own_expert, 1 - own_expert]
    chosen_of = [lax.dynamic_index_in_dim(chosen, k, 0, keepdims=False) for k in order]
    gates_of = [lax.dynamic_index_in_dim(gates, k, 0, keepdims=False) for k in order]

    if on_line:
        token_pieces = direct_gather(tokens, tokens, "tp")
    else:
        token_pieces = [([lax.all_gather(tokens, "tp", axis=1, tiled=True)], 0)]

    def gathered(weight, relay):
        if on_box:
            return box_gather(weight, "ep", relay)
        return [([lax.all_gather(weight, "ep", axis=1, tiled=True)], 0)]

    block = shared_down.shape[1]
    shared_gates = gathered(shared_gate.T, 2)
    shared_ups = gathered(shared_up.T, 6)
    shared_downs = gathered(shared_down, 4)

    window = 2 * cap // ep_count
    owner_start = jnp.arange(ep_count, dtype=jnp.int32) * tok_dev
    offsets = jnp.arange(window, dtype=jnp.int32)
    slot_rows = []
    slot_ids = []
    for ids in chosen_of:
        starts = jnp.sum((ids[None, :] < owner_start[:, None]).astype(jnp.int32), axis=1)
        rows = (starts[:, None] + offsets[None, :]).reshape(-1)
        slot_rows.append(rows.reshape(1, -1))
        hit = rows[:, None] == jnp.arange(cap, dtype=jnp.int32)[None, :]
        found = jnp.sum(jnp.where(hit, ids[None, :] + 1, 0), axis=1) - 1
        slot_ids.append(found.reshape(ep_count, window) - owner_start[:, None])
    sent_ids = jnp.stack(slot_ids, axis=1)
    owner_ids = lax.all_to_all(sent_ids, "ep", split_axis=0, concat_axis=0, tiled=True)
    owner_ids = [owner_ids[:, k].reshape(1, -1) for k in range(experts)]

    feature_at = [inner] + [(tp ^ m) * width for _, m in token_pieces]
    flag = stack_scalars([inner])
    begun = None
    for number in range(0, len(token_pieces), 2):
        batch = token_pieces[number : number + 2]
        sent = take_windows(batch, flag, owner_ids[0])
        sent = sent.reshape(ep_count, window, -1)
        rows = lax.all_to_all(sent, "ep", split_axis=0, concat_axis=0, tiled=True)
        begun = expert_hidden(
            rows.reshape(ep_count * window, -1),
            width if on_line else width * tp_count,
            stack_scalars([(tp ^ m) * width if on_line else 0 for _, m in batch]),
            slot_rows[0],
            gain,
            gate_weight,
            up_weight,
            cap,
            begun,
            number + 2 >= len(token_pieces),
        )
    part_hidden = begun[0]

    hidden_rows = part_hidden.shape[0]
    if on_line:
        pieces = direct_gather(part_hidden, part_hidden, "tp")
        hidden_of = [pieces[:2], pieces[2:]]
    else:
        whole = lax.all_gather(part_hidden, "tp", axis=0, tiled=True)
        units = hidden_rows * split
        hidden_of = [
            [([lax.dynamic_slice_in_dim(whole, k * units, units, 0)], 0)] for k in order
        ]

    def places(pieces):
        return [(ep ^ m) * block if on_box else 0 for _, m in pieces]

    early_gates, early_ups = shared_gates[:6], shared_ups[:6]
    late_gates, late_ups = shared_gates[6:], shared_ups[6:]
    in_at = feature_at + places(early_gates + early_ups)
    shared_begun = shared_in(token_pieces, early_gates, early_ups, stack_scalars(in_at), gain)
    masks = [0, 2, 1, 3] if on_line else [0]
    out_at = places(late_gates + late_ups + shared_downs)
    out_at += [(tp ^ m) * width for m in masks] if on_line else [0]
    sums = shared_out(
        shared_begun,
        late_gates,
        late_ups,
        shared_downs,
        stack_scalars(out_at),
        width if on_line else width * tp_count,
        len(masks),
    )
    if on_line:
        near = swap(sums[2], "tp", 1)
        half = (sums[1] + near[tok_dev:].astype(F32)).astype(BF16)
        shared_own = sums[0]
        shared_parts = [near, swap(half, "tp", 2)]
    else:
        shared_own = lax.psum_scatter(sums[0], "tp", scatter_dimension=1, tiled=True)
        shared_parts = []

    windows = []
    for k in range(experts):
        hidden_at = [inner] + [((tp ^ m) % split) * hidden_rows for _, m in hidden_of[k]]
        sent = expert_down(
            hidden_of[k],
            stack_scalars(hidden_at + [order[k]]),
            expert_down_weight,
            gates_of[k].reshape(1, -1),
            slot_rows[k],
        )
        sent = sent.reshape(ep_count, window, width)
        rows = lax.all_to_all(sent, "ep", split_axis=0, concat_axis=0, tiled=True)
        windows.append(rows.reshape(ep_count * window, width))
    return finish(shared_own, shared_parts, windows, owner_ids, tok_dev)


def solution(mesh):
    return jax.shard_map(
        on_device,
        mesh=mesh,
        in_specs=(
            P("ep", "tp"),
            P(),
            P("ep", "tp"),
            P("ep", "tp"),
            P("tp", "ep"),
            P("tp", "ep", None, None),
            P("tp", "ep", None, None),
            P("ep", None, "tp"),
            P("ep", None),
            P("ep", None),
        ),
        out_specs=P("ep", "tp"),
        check_vma=False,
    )
```

time: 248 us -> 254 us (1.024)
  the two profiles are of different devices: /device:TPU:10 before, /device:TPU:0 now
where the time goes in v2:
time: 254 us; the launch traced here: 253 us
  waiting for transfers between devices  125 us (49%)
  starting transfers between devices  62.1 us (24%)
  Pallas kernels  46 us (18%)
  local copies, waits for them, and re-layouts  14.6 us (6%)
  other arithmetic  4.94 us (2%)
    ppermute x29, waiting for transfers between devices, swap(): return lax.ppermute(x, axis, [(i, i ^ mask) for i in range(count)])  121 us
    ppermute x29, starting transfers between devices, swap(): return lax.ppermute(x, axis, [(i, i ^ mask) for i in range(count)])  42.7 us
    all_to_all x4, starting transfers between devices, on_device(): rows = lax.all_to_all(sent, 'ep', split_axis=0, concat_axis=0, tiled=True)  15.7 us
    pallas_call x2, Pallas kernels, expert_hidden(): kernel(body, result, [SMEM_SPEC, VMEM_SPEC, VMEM_SPEC] + [HBM_SPEC] * 2 +...  12.2 us
    unnamed x60, local copies, waits for them, and re-layouts  9.81 us
    pallas_call x2, Pallas kernels, expert_down(): kernel(body, jax.ShapeDtypeStruct((slots, width), BF16), [SMEM_SPEC, VMEM...  9.63 us
    pallas_call x2, Pallas kernels, take_windows(): kernel(body, jax.ShapeDtypeStruct((slots, width * len(pieces)), BF16), [S...  7.27 us
    pallas_call x1, Pallas kernels, shared_out(): kernel(body, [jax.ShapeDtypeStruct((tok_dev, width), F32)] * min(blocks,...  7 us
  transfers between devices with their start and end apart: 34, of which 9 were waited for; matrix products, arithmetic and copies ran while one was open for 4% of the time, Pallas kernels for 15%

profile of v2, /device:TPU:0, one launch (start us, length us, event | category | flops | bytes accessed | tf_op | source)
XLA Modules:
  0.0 253.2 jit_solution(17428527382986582376)
XLA Ops:
  0.0 3.1 %collective-permute-start = (bf16[384,512]{1,0:T(8,128)(2,1)}, bf16[384,512]{1,0:T(8,128)(2,1)S(1)}, u32[]{:S(2)}, u32[]{:S(2)}) collective-permute-start(bf16[384,512]{1,0:T(8,128)(2,1)} %refs_0_.3), channel_id=1, source_target_pairs={{0,8},{8,0},{16,24},{24,16},{1,9},{9,1},{17,25},{25,17},{2,10},{10... | collective-permute-start | bytes 1179656 | tf_op jit(solution)/shard_map/ppermute | solution.py:22
  5.7 3.7 %all-to-all-start = ((s32[8,2,96]{2,1,0:T(2,128)}), s32[8,2,96]{2,1,0:T(2,128)S(1)}, u32[]{:S(2)}, u32[]{:S(2)}) async-start(s32[8,2,96]{2,1,0:T(2,128)} %pad_add_fusion), calls=%async_computation | async-start | bytes 16384 | tf_op jit(solution)/shard_map/all_to_all | solution.py:391
  9.5 4.7 %all-to-all-done = s32[8,2,96]{2,1,0:T(2,128)S(1)} async-done(((s32[8,2,96]{2,1,0:T(2,128)}), s32[8,2,96]{2,1,0:T(2,128)S(1)}, u32[]{:S(2)}, u32[]{:S(2)}) %all-to-all-start) | async-done | bytes 6176 | tf_op jit(solution)/shard_map/all_to_all | solution.py:391
  15.6 3.6 %shard_map.103 = bf16[768,1024]{1,0:T(8,128)(2,1)} custom-call(s32[1]{0:T(128)} %bitcast.12.pos_ref, s32[1,768]{1,0:T(1,128)} %reshape_squeeze.6.ids_ref.refs_4_, bf16[384,512]{1,0:T(8,128)(2,1)} %refs_0_.3, bf16[384,512]{1,0:T(8,128)(2,1)} %copy-done.7), custom_call_target="tpu_custom_call" | custom-call | tf_op jit(solution)/shard_map/pallas_call | solution.py:119
  19.2 3.7 %all-to-all-start.2 = ((bf16[8,96,1024]{2,1,0:T(8,128)(2,1)}), bf16[8,96,1024]{2,1,0:T(8,128)(2,1)S(1)}, u32[]{:S(2)}, u32[]{:S(2)}) async-start(bf16[8,96,1024]{2,1,0:T(8,128)(2,1)} %bitcast.37), calls=%async_computation.2 | async-start | bytes 3145728 | tf_op jit(solution)/shard_map/all_to_all | solution.py:401
  23.0 2.6 %collective-permute-start.1 = (bf16[384,512]{1,0:T(8,128)(2,1)S(1)}, bf16[384,512]{1,0:T(8,128)(2,1)S(1)}, u32[]{:S(2)}, u32[]{:S(2)}) collective-permute-start(bf16[384,512]{1,0:T(8,128)(2,1)S(1)} %copy-done.6), channel_id=1, source_target_pairs={{0,16},{8,24},{16,0},{24,8},{1,17},{9,25},{17,1},{25,9},{2,18},{10... | collective-permute-start | bytes 1179656 | tf_op jit(solution)/shard_map/ppermute | solution.py:22
  25.8 26.2 %collective-permute-done.1.refs_2_.refs_0_ = bf16[384,512]{1,0:T(8,128)(2,1)S(1)} collective-permute-done((bf16[384,512]{1,0:T(8,128)(2,1)S(1)}, bf16[384,512]{1,0:T(8,128)(2,1)S(1)}, u32[]{:S(2)}, u32[]{:S(2)}) %collective-permute-start.1) | collective-permute-done | bytes 393248 | tf_op jit(solution)/shard_map/ppermute | solution.py:22
  53.6 3.7 %shard_map.102 = bf16[768,1024]{1,0:T(8,128)(2,1)} custom-call(s32[1]{0:T(128)} %bitcast.12.pos_ref, s32[1,768]{1,0:T(1,128)} %reshape_squeeze.6.ids_ref.refs_4_, bf16[384,512]{1,0:T(8,128)(2,1)} %copy-done.8, bf16[384,512]{1,0:T(8,128)(2,1)} %copy-done.9), custom_call_target="tpu_custom_call" | custom-call | tf_op jit(solution)/shard_map/pallas_call | solution.py:119
  58.4 3.9 %all-to-all-start.1 = ((bf16[8,96,1024]{2,1,0:T(8,128)(2,1)}), bf16[8,96,1024]{2,1,0:T(8,128)(2,1)S(1)}, u32[]{:S(2)}, u32[]{:S(2)}) async-start(bf16[8,96,1024]{2,1,0:T(8,128)(2,1)} %bitcast.36), calls=%async_computation.1 | async-start | bytes 3145728 | tf_op jit(solution)/shard_map/all_to_all | solution.py:401
  62.2 2.0 collective-permute-start.3
  64.3 1.5 collective-permute-start.4
  66.3 24.3 %collective-permute-done.3.refs_5_ = bf16[704,256]{1,0:T(8,128)(2,1)S(1)} collective-permute-done((bf16[704,256]{1,0:T(8,128)(2,1)}, bf16[704,256]{1,0:T(8,128)(2,1)S(1)}, u32[]{:S(2)}, u32[]{:S(2)}) %collective-permute-start.3) | collective-permute-done | bytes 360480 | tf_op jit(solution)/shard_map/ppermute | solution.py:22
  90.7 1.5 collective-permute-start.15
  92.2 1.5 collective-permute-start.17
  93.7 4.8 %collective-permute-done.8.refs_11_ = bf16[704,256]{1,0:T(8,128)(2,1)} collective-permute-done((bf16[704,256]{1,0:T(8,128)(2,1)}, bf16[704,256]{1,0:T(8,128)(2,1)}, u32[]{:S(2)}, u32[]{:S(2)}) %collective-permute-start.8) | collective-permute-done | bytes 360480 | tf_op jit(solution)/shard_map/ppermute | solution.py:22
  98.5 1.5 collective-permute-start.18
  100.5 6.6 %collective-permute-done.15.refs_2_ = bf16[704,256]{1,0:T(8,128)(2,1)S(1)} collective-permute-done((bf16[704,256]{1,0:T(8,128)(2,1)}, bf16[704,256]{1,0:T(8,128)(2,1)S(1)}, u32[]{:S(2)}, u32[]{:S(2)}) %collective-permute-start.15) | collective-permute-done | bytes 360480 | tf_op jit(solution)/shard_map/ppermute | solution.py:22
  107.1 6.2 %collective-permute-done.17.refs_5_ = bf16[704,256]{1,0:T(8,128)(2,1)S(1)} collective-permute-done((bf16[704,256]{1,0:T(8,128)(2,1)S(1)}, bf16[704,256]{1,0:T(8,128)(2,1)S(1)}, u32[]{:S(2)}, u32[]{:S(2)}) %collective-permute-start.17) | collective-permute-done | bytes 360480 | tf_op jit(solution)/shard_map/ppermute | solution.py:22
  119.3 5.8 %shard_map.104 = (f32[704,384]{1,0:T(8,128)}, f32[704,384]{1,0:T(8,128)}, f32[1,384]{1,0:T(1,128)}) custom-call(s32[2]{0:T(128)} %pad_add_fusion.3.pos_ref, s32[1,768]{1,0:T(1,128)} %add.121.slot_ref, f32[1,2048]{1,0:T(1,128)} %bitcast.53, bf16[704,2048]{1,0:T(8,128)(2,1)} %bitcast.32, bf16[704,2048]{1,0:T(8,128)(2,1)} %bitcast.34, bf16[768,1024]{1,0:T(8,128)(2,1)} %bitcast.38), custom_call_target="tpu_custom_call" | custom-call | tf_op jit(solution)/shard_map/pallas_call | solution.py:179
  126.3 6.4 %shard_map.105.refs_0_ = bf16[704,384]{1,0:T(8,128)(2,1)} custom-call(s32[2]{0:T(128)} %pad_add_fusion.2.pos_ref, s32[1,768]{1,0:T(1,128)} %add.121.slot_ref, f32[1,2048]{1,0:T(1,128)} %bitcast.54, bf16[704,2048]{1,0:T(8,128)(2,1)} %bitcast.33, bf16[704,2048]{1,0:T(8,128)(2,1)} %bitcast.35, bf16[768,1024]{1,0:T(8,128)(2,1)} %bitcast.39, ...), custom_call_target="tpu_custom_call" | custom-call | tf_op jit(solution)/shard_map/pallas_call | solution.py:179
  132.7 8.2 %collective-permute-start.26 = (bf16[704,384]{1,0:T(8,128)(2,1)}, bf16[704,384]{1,0:T(8,128)(2,1)S(1)}, u32[]{:S(2)}, u32[]{:S(2)}) collective-permute-start(bf16[704,384]{1,0:T(8,128)(2,1)} %shard_map.105.refs_0_), channel_id=1, source_target_pairs={{0,8},{8,0},{16,24},{24,16},{1,9},{9,1},{17,25},{25,17},{2,10},{10... | collective-permute-start | bytes 1622024 | tf_op jit(solution)/shard_map/ppermute | solution.py:22
  143.9 6.4 %shard_map.100 = (bf16[384,2048]{1,0:T(8,128)(2,1)}, f32[384,704]{1,0:T(8,128)}, f32[384,704]{1,0:T(8,128)}) custom-call(s32[17]{0:T(128)} %stack.124.pos_ref, f32[1,2048]{1,0:T(1,128)} %bitcast.55, bf16[384,512]{1,0:T(8,128)(2,1)} %refs_0_.3, bf16[384,512]{1,0:T(8,128)(2,1)} %copy-done.7, bf16[384,512]{1,0:T(8,128)(2,1)} %copy-done.8, ...), custom_call_target="tpu_custom_call" | custom-call | tf_op jit(solution)/shard_map/pallas_call | solution.py:253
  151.4 7.0 %shard_map.101 = (f32[384,512]{1,0:T(8,128)}, f32[384,512]{1,0:T(8,128)}, bf16[768,512]{1,0:T(8,128)(2,1)}) custom-call(s32[16]{0:T(128)} %stack.121.pos_ref, bf16[384,2048]{1,0:T(8,128)(2,1)} %get-tuple-element.14.x_ref, f32[384,704]{1,0:T(8,128)} %get-tuple-element.15.gate_in, f32[384,704]{1,0:T(8,128)} %get-tuple-element.16.up_in, ...), custom_call_target="tpu_custom_call" | custom-call | tf_op jit(solution)/shard_map/pallas_call | solution.py:295
  159.9 4.8 %shard_map.106 = bf16[768,512]{1,0:T(8,128)(2,1)} custom-call(s32[4]{0:T(128)} %pad_add_fusion.1.pos_ref, f32[1,384]{1,0:T(1,128)} %get-tuple-element.32.gate_ref, s32[1,768]{1,0:T(1,128)} %add.121.slot_ref, bf16[2,1408,512]{2,1,0:T(8,128)(2,1)} %down_hbm.3, bf16[704,384]{1,0:T(8,128)(2,1)} %shard_map.105.refs_0_, bf16[704,384]{1,0:T(8,128)(2,1)} %copy-done.11), custom_call_target="tpu_custom_call" | custom-call | tf_op jit(solution)/shard_map/pallas_call | solution.py:212
  164.7 3.9 %all-to-all-start.3 = ((bf16[8,96,512]{2,1,0:T(8,128)(2,1)}), bf16[8,96,512]{2,1,0:T(8,128)(2,1)S(1)}, u32[]{:S(2)}, u32[]{:S(2)}) async-start(bf16[8,96,512]{2,1,0:T(8,128)(2,1)} %bitcast.42), calls=%async_computation.3 | async-start | bytes 1572864 | tf_op jit(solution)/shard_map/all_to_all | solution.py:466
  168.6 3.1 %collective-permute-start.27 = (bf16[704,384]{1,0:T(8,128)(2,1)S(1)}, bf16[704,384]{1,0:T(8,128)(2,1)S(1)}, u32[]{:S(2)}, u32[]{:S(2)}) collective-permute-start(bf16[704,384]{1,0:T(8,128)(2,1)S(1)} %copy-done.4), channel_id=1, source_target_pairs={{0,16},{8,24},{16,0},{24,8},{1,17},{9,25},{17,1},{25,9},{2,18},{10... | collective-permute-start | bytes 1622024 | tf_op jit(solution)/shard_map/ppermute | solution.py:22
  174.3 33.8 %collective-permute-done.27.refs_0_ = bf16[704,384]{1,0:T(8,128)(2,1)S(1)} collective-permute-done((bf16[704,384]{1,0:T(8,128)(2,1)S(1)}, bf16[704,384]{1,0:T(8,128)(2,1)S(1)}, u32[]{:S(2)}, u32[]{:S(2)}) %collective-permute-start.27) | collective-permute-done | bytes 540704 | tf_op jit(solution)/shard_map/ppermute | solution.py:22
  209.1 4.8 %shard_map.107 = bf16[768,512]{1,0:T(8,128)(2,1)} custom-call(s32[4]{0:T(128)} %pad_add_fusion.4.pos_ref, f32[1,384]{1,0:T(1,128)} %get-tuple-element.31.gate_ref, s32[1,768]{1,0:T(1,128)} %add.132.slot_ref, bf16[2,1408,512]{2,1,0:T(8,128)(2,1)} %down_hbm.3, bf16[704,384]{1,0:T(8,128)(2,1)} %copy-done.12, bf16[704,384]{1,0:T(8,128)(2,1)} %copy-done.13), custom_call_target="tpu_custom_call" | custom-call | tf_op jit(solution)/shard_map/pallas_call | solution.py:212
  214.0 4.2 %all-to-all-start.4 = ((bf16[8,96,512]{2,1,0:T(8,128)(2,1)}), bf16[8,96,512]{2,1,0:T(8,128)(2,1)S(1)}, u32[]{:S(2)}, u32[]{:S(2)}) async-start(bf16[8,96,512]{2,1,0:T(8,128)(2,1)} %bitcast.43), calls=%async_computation.4 | async-start | bytes 1572864 | tf_op jit(solution)/shard_map/all_to_all | solution.py:466
  218.3 12.2 %collective-permute-start.25 = (bf16[384,512]{1,0:T(8,128)(2,1)S(1)}, bf16[384,512]{1,0:T(8,128)(2,1)S(1)}, u32[]{:S(2)}, u32[]{:S(2)}) collective-permute-start(bf16[384,512]{1,0:T(8,128)(2,1)S(1)} %add_convert_fusion), channel_id=1, source_target_pairs={{0,16},{8,24},{16,0},{24,8},{1,17},{9,25},{17,1},{25,9},{2,18},{10... | collective-permute-start | bytes 1179656 | tf_op jit(solution)/shard_map/ppermute | solution.py:22
  231.1 17.6 %collective-permute-done.25.refs_1_ = bf16[384,512]{1,0:T(8,128)(2,1)S(1)} collective-permute-done((bf16[384,512]{1,0:T(8,128)(2,1)S(1)}, bf16[384,512]{1,0:T(8,128)(2,1)S(1)}, u32[]{:S(2)}, u32[]{:S(2)}) %collective-permute-start.25) | collective-permute-done | bytes 393248 | tf_op jit(solution)/shard_map/ppermute | solution.py:22
  249.7 3.5 %shard_map.108 = bf16[384,512]{1,0:T(8,128)(2,1)} custom-call(f32[384,512]{1,0:T(8,128)} %get-tuple-element.17.own_ref, bf16[768,512]{1,0:T(8,128)(2,1)} %copy-done.5, bf16[384,512]{1,0:T(8,128)(2,1)} %copy-done.14, bf16[768,512]{1,0:T(8,128)(2,1)} %bitcast.40, bf16[768,512]{1,0:T(8,128)(2,1)} %bitcast.41, s32[1,768]{1,0:T(1,128)} %reshape_squeeze.6.ids_ref.refs_4_, ...), custom_call_target="tpu_custom_call" | custom-call | tf_op jit(solution)/shard_map/pallas_call | solution.py:323
  (132 shorter events, 26.0 us)
Async XLA Ops:
  0.0 14.9 %collective-permute-start = (bf16[384,512]{1,0:T(8,128)(2,1)}, bf16[384,512]{1,0:T(8,128)(2,1)S(1)}, u32[]{:S(2)}, u32[]{:S(2)}) collective-permute-start(bf16[384,512]{1,0:T(8,128)(2,1)} %refs_0_.3), channel_id=1, source_target_pairs={{0,8},{8,0},{16,24},{24,16},{1,9},{9,1},{17,25},{25,17},{2,10},{10... | collective-permute-start | bytes 1179656 | tf_op jit(solution)/shard_map/ppermute | solution.py:22
  19.2 38.0 %all-to-all-start.2 = ((bf16[8,96,1024]{2,1,0:T(8,128)(2,1)}), bf16[8,96,1024]{2,1,0:T(8,128)(2,1)S(1)}, u32[]{:S(2)}, u32[]{:S(2)}) async-start(bf16[8,96,1024]{2,1,0:T(8,128)(2,1)} %bitcast.37), calls=%async_computation.2 | async-start | bytes 3145728 | tf_op jit(solution)/shard_map/all_to_all | solution.py:401
  23.0 29.1 %collective-permute-start.1 = (bf16[384,512]{1,0:T(8,128)(2,1)S(1)}, bf16[384,512]{1,0:T(8,128)(2,1)S(1)}, u32[]{:S(2)}, u32[]{:S(2)}) collective-permute-start(bf16[384,512]{1,0:T(8,128)(2,1)S(1)} %copy-done.6), channel_id=1, source_target_pairs={{0,16},{8,24},{16,0},{24,8},{1,17},{9,25},{17,1},{25,9},{2,18},{10... | collective-permute-start | bytes 1179656 | tf_op jit(solution)/shard_map/ppermute | solution.py:22
  25.6 26.5 %collective-permute-start.2 = (bf16[384,512]{1,0:T(8,128)(2,1)S(1)}, bf16[384,512]{1,0:T(8,128)(2,1)S(1)}, u32[]{:S(2)}, u32[]{:S(2)}) collective-permute-start(bf16[384,512]{1,0:T(8,128)(2,1)S(1)} %copy-done.6), channel_id=1, source_target_pairs={{0,24},{8,16},{16,8},{24,0},{1,25},{9,17},{17,9},{25,1},{2,26},{10... | collective-permute-start | bytes 1179656 | tf_op jit(solution)/shard_map/ppermute | solution.py:22
  58.4 66.7 %all-to-all-start.1 = ((bf16[8,96,1024]{2,1,0:T(8,128)(2,1)}), bf16[8,96,1024]{2,1,0:T(8,128)(2,1)S(1)}, u32[]{:S(2)}, u32[]{:S(2)}) async-start(bf16[8,96,1024]{2,1,0:T(8,128)(2,1)} %bitcast.36), calls=%async_computation.1 | async-start | bytes 3145728 | tf_op jit(solution)/shard_map/all_to_all | solution.py:401
  62.2 28.4 %collective-permute-start.3 = (bf16[704,256]{1,0:T(8,128)(2,1)}, bf16[704,256]{1,0:T(8,128)(2,1)S(1)}, u32[]{:S(2)}, u32[]{:S(2)}) collective-permute-start(bf16[704,256]{1,0:T(8,128)(2,1)} %bitcast.44), channel_id=1, source_target_pairs={{0,2},{1,3},{2,0},{3,1},{4,6},{5,7},{6,4},{7,5},{8,10},{9,11},{10,... | collective-permute-start | bytes 1081352 | tf_op jit(solution)/shard_map/ppermute | solution.py:22
  64.3 26.4 %collective-permute-start.4 = (bf16[704,256]{1,0:T(8,128)(2,1)}, bf16[704,256]{1,0:T(8,128)(2,1)}, u32[]{:S(2)}, u32[]{:S(2)}) collective-permute-start(bf16[704,256]{1,0:T(8,128)(2,1)} %bitcast.45), channel_id=1, source_target_pairs={{0,4},{1,5},{2,6},{3,7},{4,0},{5,1},{6,2},{7,3},{8,12},{9,13},{10,... | collective-permute-start | bytes 1081352 | tf_op jit(solution)/shard_map/ppermute | solution.py:22
  65.7 26.5 %collective-permute-start.5 = (bf16[704,256]{1,0:T(8,128)(2,1)}, bf16[704,256]{1,0:T(8,128)(2,1)}, u32[]{:S(2)}, u32[]{:S(2)}) collective-permute-start(bf16[704,256]{1,0:T(8,128)(2,1)} %bitcast.46), channel_id=1, source_target_pairs={{0,1},{1,0},{2,3},{3,2},{4,5},{5,4},{6,7},{7,6},{8,9},{9,8},{10,11... | collective-permute-start | bytes 1081352 | tf_op jit(solution)/shard_map/ppermute | solution.py:22
  65.7 32.8 %collective-permute-start.8 = (bf16[704,256]{1,0:T(8,128)(2,1)}, bf16[704,256]{1,0:T(8,128)(2,1)}, u32[]{:S(2)}, u32[]{:S(2)}) collective-permute-start(bf16[704,256]{1,0:T(8,128)(2,1)} %bitcast.48), channel_id=1, source_target_pairs={{0,2},{1,3},{2,0},{3,1},{4,6},{5,7},{6,4},{7,5},{8,10},{9,11},{10,... | collective-permute-start | bytes 1081352 | tf_op jit(solution)/shard_map/ppermute | solution.py:22
  66.3 33.7 %collective-permute-start.9 = (bf16[704,256]{1,0:T(8,128)(2,1)}, bf16[704,256]{1,0:T(8,128)(2,1)}, u32[]{:S(2)}, u32[]{:S(2)}) collective-permute-start(bf16[704,256]{1,0:T(8,128)(2,1)} %bitcast.49), channel_id=1, source_target_pairs={{0,4},{1,5},{2,6},{3,7},{4,0},{5,1},{6,2},{7,3},{8,12},{9,13},{10,... | collective-permute-start | bytes 1081352 | tf_op jit(solution)/shard_map/ppermute | solution.py:22
  90.7 9.3 %collective-permute-start.10 = (bf16[704,256]{1,0:T(8,128)(2,1)}, bf16[704,256]{1,0:T(8,128)(2,1)S(1)}, u32[]{:S(2)}, u32[]{:S(2)}) collective-permute-start(bf16[704,256]{1,0:T(8,128)(2,1)} %bitcast.50), channel_id=1, source_target_pairs={{0,1},{1,0},{2,3},{3,2},{4,5},{5,4},{6,7},{7,6},{8,9},{9,8},{10,11... | collective-permute-start | bytes 1081352 | tf_op jit(solution)/shard_map/ppermute | solution.py:22
  90.7 16.4 %collective-permute-start.15 = (bf16[704,256]{1,0:T(8,128)(2,1)}, bf16[704,256]{1,0:T(8,128)(2,1)S(1)}, u32[]{:S(2)}, u32[]{:S(2)}) collective-permute-start(bf16[704,256]{1,0:T(8,128)(2,1)} %bitcast.51), channel_id=1, source_target_pairs={{0,6},{1,7},{2,4},{3,5},{4,2},{5,3},{6,0},{7,1},{8,14},{9,15},{10,... | collective-permute-start | bytes 1081352 | tf_op jit(solution)/shard_map/ppermute | solution.py:22
  92.2 21.1 %collective-permute-start.17 = (bf16[704,256]{1,0:T(8,128)(2,1)S(1)}, bf16[704,256]{1,0:T(8,128)(2,1)S(1)}, u32[]{:S(2)}, u32[]{:S(2)}) collective-permute-start(bf16[704,256]{1,0:T(8,128)(2,1)S(1)} %copy-done.15), channel_id=1, source_target_pairs={{0,2},{1,3},{2,0},{3,1},{4,6},{5,7},{6,4},{7,5},{8,10},{9,11},{10,... | collective-permute-start | bytes 1081352 | tf_op jit(solution)/shard_map/ppermute | solution.py:22
  98.5 15.7 %collective-permute-start.18 = (bf16[704,256]{1,0:T(8,128)(2,1)S(1)}, bf16[704,256]{1,0:T(8,128)(2,1)S(1)}, u32[]{:S(2)}, u32[]{:S(2)}) collective-permute-start(bf16[704,256]{1,0:T(8,128)(2,1)S(1)} %copy-done.15), channel_id=1, source_target_pairs={{0,4},{1,5},{2,6},{3,7},{4,0},{5,1},{6,2},{7,3},{8,12},{9,13},{10,... | collective-permute-start | bytes 1081352 | tf_op jit(solution)/shard_map/ppermute | solution.py:22
  100.0 14.2 %collective-permute-start.19 = (bf16[704,256]{1,0:T(8,128)(2,1)S(1)}, bf16[704,256]{1,0:T(8,128)(2,1)S(1)}, u32[]{:S(2)}, u32[]{:S(2)}) collective-permute-start(bf16[704,256]{1,0:T(8,128)(2,1)S(1)} %copy-done.15), channel_id=1, source_target_pairs={{0,1},{1,0},{2,3},{3,2},{4,5},{5,4},{6,7},{7,6},{8,9},{9,8},{10,11... | collective-permute-start | bytes 1081352 | tf_op jit(solution)/shard_map/ppermute | solution.py:22
  100.0 14.8 %collective-permute-start.6 = (bf16[704,256]{1,0:T(8,128)(2,1)S(1)}, bf16[704,256]{1,0:T(8,128)(2,1)S(1)}, u32[]{:S(2)}, u32[]{:S(2)}) collective-permute-start(bf16[704,256]{1,0:T(8,128)(2,1)S(1)} %collective-permute-done.3.refs_5_), channel_id=1, source_target_pairs={{0,1},{1,0},{2,3},{3,2},{4,5},{5,4},{6,7},{7,6},{8,9},{9,8},{10,11... | collective-permute-start | bytes 1081352 | tf_op jit(solution)/shard_map/ppermute | solution.py:22
  113.3 19.4 %collective-permute-start.11 = (bf16[704,256]{1,0:T(8,128)(2,1)}, bf16[704,256]{1,0:T(8,128)(2,1)}, u32[]{:S(2)}, u32[]{:S(2)}) collective-permute-start(bf16[704,256]{1,0:T(8,128)(2,1)} %collective-permute-done.8.refs_11_), channel_id=1, source_target_pairs={{0,1},{1,0},{2,3},{3,2},{4,5},{5,4},{6,7},{7,6},{8,9},{9,8},{10,11... | collective-permute-start | bytes 1081352 | tf_op jit(solution)/shard_map/ppermute | solution.py:22
  114.2 26.8 %collective-permute-start.12 = (bf16[704,256]{1,0:T(8,128)(2,1)}, bf16[704,256]{1,0:T(8,128)(2,1)}, u32[]{:S(2)}, u32[]{:S(2)}) collective-permute-start(bf16[704,256]{1,0:T(8,128)(2,1)} %collective-permute-done.9.refs_12_), channel_id=1, source_target_pairs={{0,1},{1,0},{2,3},{3,2},{4,5},{5,4},{6,7},{7,6},{8,9},{9,8},{10,11... | collective-permute-start | bytes 1081352 | tf_op jit(solution)/shard_map/ppermute | solution.py:22
  114.2 26.8 %collective-permute-start.13 = (bf16[704,256]{1,0:T(8,128)(2,1)}, bf16[704,256]{1,0:T(8,128)(2,1)S(1)}, u32[]{:S(2)}, u32[]{:S(2)}) collective-permute-start(bf16[704,256]{1,0:T(8,128)(2,1)} %collective-permute-done.4.refs_6_), channel_id=1, source_target_pairs={{0,2},{1,3},{2,0},{3,1},{4,6},{5,7},{6,4},{7,5},{8,10},{9,11},{10,... | collective-permute-start | bytes 1081352 | tf_op jit(solution)/shard_map/ppermute | solution.py:22
  114.8 26.7 %collective-permute-start.16 = (bf16[704,256]{1,0:T(8,128)(2,1)S(1)}, bf16[704,256]{1,0:T(8,128)(2,1)}, u32[]{:S(2)}, u32[]{:S(2)}) collective-permute-start(bf16[704,256]{1,0:T(8,128)(2,1)S(1)} %collective-permute-done.15.refs_2_), channel_id=1, source_target_pairs={{0,1},{1,0},{2,3},{3,2},{4,5},{5,4},{6,7},{7,6},{8,9},{9,8},{10,11... | collective-permute-start | bytes 1081352 | tf_op jit(solution)/shard_map/ppermute | solution.py:22
  116.3 25.3 %collective-permute-start.22 = (bf16[704,256]{1,0:T(8,128)(2,1)S(1)}, bf16[704,256]{1,0:T(8,128)(2,1)}, u32[]{:S(2)}, u32[]{:S(2)}) collective-permute-start(bf16[704,256]{1,0:T(8,128)(2,1)S(1)} %collective-permute-done.17.refs_5_), channel_id=1, source_target_pairs={{0,4},{1,5},{2,6},{3,7},{4,0},{5,1},{6,2},{7,3},{8,12},{9,13},{10,... | collective-permute-start | bytes 1081352 | tf_op jit(solution)/shard_map/ppermute | solution.py:22
  132.7 26.4 %collective-permute-start.26 = (bf16[704,384]{1,0:T(8,128)(2,1)}, bf16[704,384]{1,0:T(8,128)(2,1)S(1)}, u32[]{:S(2)}, u32[]{:S(2)}) collective-permute-start(bf16[704,384]{1,0:T(8,128)(2,1)} %shard_map.105.refs_0_), channel_id=1, source_target_pairs={{0,8},{8,0},{16,24},{24,16},{1,9},{9,1},{17,25},{25,17},{2,10},{10... | collective-permute-start | bytes 1622024 | tf_op jit(solution)/shard_map/ppermute | solution.py:22
  141.0 9.3 %collective-permute-start.20 = (bf16[704,256]{1,0:T(8,128)(2,1)S(1)}, bf16[704,256]{1,0:T(8,128)(2,1)S(1)}, u32[]{:S(2)}, u32[]{:S(2)}) collective-permute-start(bf16[704,256]{1,0:T(8,128)(2,1)S(1)} %collective-permute-done.17.refs_5_), channel_id=1, source_target_pairs={{0,1},{1,0},{2,3},{3,2},{4,5},{5,4},{6,7},{7,6},{8,9},{9,8},{10,11... | collective-permute-start | bytes 1081352 | tf_op jit(solution)/shard_map/ppermute | solution.py:22
  141.0 9.3 %collective-permute-start.21 = (bf16[704,256]{1,0:T(8,128)(2,1)S(1)}, bf16[704,256]{1,0:T(8,128)(2,1)S(1)}, u32[]{:S(2)}, u32[]{:S(2)}) collective-permute-start(bf16[704,256]{1,0:T(8,128)(2,1)S(1)} %collective-permute-done.18.refs_6_), channel_id=1, source_target_pairs={{0,1},{1,0},{2,3},{3,2},{4,5},{5,4},{6,7},{7,6},{8,9},{9,8},{10,11... | collective-permute-start | bytes 1081352 | tf_op jit(solution)/shard_map/ppermute | solution.py:22
  141.6 8.8 %collective-permute-start.14 = (bf16[704,256]{1,0:T(8,128)(2,1)S(1)}, bf16[704,256]{1,0:T(8,128)(2,1)S(1)}, u32[]{:S(2)}, u32[]{:S(2)}) collective-permute-start(bf16[704,256]{1,0:T(8,128)(2,1)S(1)} %collective-permute-done.13.refs_0_), channel_id=1, source_target_pairs={{0,1},{1,0},{2,3},{3,2},{4,5},{5,4},{6,7},{7,6},{8,9},{9,8},{10,11... | collective-permute-start | bytes 1081352 | tf_op jit(solution)/shard_map/ppermute | solution.py:22
  141.6 8.7 %collective-permute-start.23 = (bf16[704,256]{1,0:T(8,128)(2,1)}, bf16[704,256]{1,0:T(8,128)(2,1)S(1)}, u32[]{:S(2)}, u32[]{:S(2)}) collective-permute-start(bf16[704,256]{1,0:T(8,128)(2,1)} %collective-permute-done.22.refs_10_), channel_id=1, source_target_pairs={{0,1},{1,0},{2,3},{3,2},{4,5},{5,4},{6,7},{7,6},{8,9},{9,8},{10,11... | collective-permute-start | bytes 1081352 | tf_op jit(solution)/shard_map/ppermute | solution.py:22
  158.4 59.8 %collective-permute-start.24 = (bf16[768,512]{1,0:T(8,128)(2,1)}, bf16[768,512]{1,0:T(8,128)(2,1)S(1)}, u32[]{:S(2)}, u32[]{:S(2)}) collective-permute-start(bf16[768,512]{1,0:T(8,128)(2,1)} %get-tuple-element.18), channel_id=1, source_target_pairs={{0,8},{8,0},{16,24},{24,16},{1,9},{9,1},{17,25},{25,17},{2,10},{10... | collective-permute-start | bytes 2359304 | tf_op jit(solution)/shard_map/ppermute | solution.py:22
  164.7 49.2 %all-to-all-start.3 = ((bf16[8,96,512]{2,1,0:T(8,128)(2,1)}), bf16[8,96,512]{2,1,0:T(8,128)(2,1)S(1)}, u32[]{:S(2)}, u32[]{:S(2)}) async-start(bf16[8,96,512]{2,1,0:T(8,128)(2,1)} %bitcast.42), calls=%async_computation.3 | async-start | bytes 1572864 | tf_op jit(solution)/shard_map/all_to_all | solution.py:466
  168.6 39.5 %collective-permute-start.27 = (bf16[704,384]{1,0:T(8,128)(2,1)S(1)}, bf16[704,384]{1,0:T(8,128)(2,1)S(1)}, u32[]{:S(2)}, u32[]{:S(2)}) collective-permute-start(bf16[704,384]{1,0:T(8,128)(2,1)S(1)} %copy-done.4), channel_id=1, source_target_pairs={{0,16},{8,24},{16,0},{24,8},{1,17},{9,25},{17,1},{25,9},{2,18},{10... | collective-permute-start | bytes 1622024 | tf_op jit(solution)/shard_map/ppermute | solution.py:22
  171.8 36.3 %collective-permute-start.28 = (bf16[704,384]{1,0:T(8,128)(2,1)S(1)}, bf16[704,384]{1,0:T(8,128)(2,1)S(1)}, u32[]{:S(2)}, u32[]{:S(2)}) collective-permute-start(bf16[704,384]{1,0:T(8,128)(2,1)S(1)} %copy-done.4), channel_id=1, source_target_pairs={{0,24},{8,16},{16,8},{24,0},{1,25},{9,17},{17,9},{25,1},{2,26},{10... | collective-permute-start | bytes 1622024 | tf_op jit(solution)/shard_map/ppermute | solution.py:22
  214.0 34.7 %all-to-all-start.4 = ((bf16[8,96,512]{2,1,0:T(8,128)(2,1)}), bf16[8,96,512]{2,1,0:T(8,128)(2,1)S(1)}, u32[]{:S(2)}, u32[]{:S(2)}) async-start(bf16[8,96,512]{2,1,0:T(8,128)(2,1)} %bitcast.43), calls=%async_computation.4 | async-start | bytes 1572864 | tf_op jit(solution)/shard_map/all_to_all | solution.py:466
  218.3 30.4 %collective-permute-start.25 = (bf16[384,512]{1,0:T(8,128)(2,1)S(1)}, bf16[384,512]{1,0:T(8,128)(2,1)S(1)}, u32[]{:S(2)}, u32[]{:S(2)}) collective-permute-start(bf16[384,512]{1,0:T(8,128)(2,1)S(1)} %add_convert_fusion), channel_id=1, source_target_pairs={{0,16},{8,24},{16,0},{24,8},{1,17},{9,25},{17,1},{25,9},{2,18},{10... | collective-permute-start | bytes 1179656 | tf_op jit(solution)/shard_map/ppermute | solution.py:22
  (32 other events, 261.1 us)

commit v3 on v2

--- a/solution.py
+++ b/solution.py
@@ -135,8 +135,12 @@
     prior = 3 if begun else 0
 
     def body(pos_ref, slot_ref, gain_ref, gate_hbm, up_hbm, window_ref, *refs):
-        outs = refs[prior:-4]
-        gate_ref, up_ref, x_ref, sems = refs[-4:]
+        outs = refs[prior : prior + len(result)]
+        gate_ref, up_ref, x_ref, sems, *sums = refs[prior + len(result) :]
+        sum_copies = [
+            pltpu.make_async_copy(refs[n], sums[n], sems.at[2 * parts + n])
+            for n in range(len(sums))
+        ]
         cols = [pl.multiple_of(pos_ref[n], 128) for n in range(parts)]
         copies = []
         for matrix, (source, target) in enumerate(((gate_hbm, gate_ref), (up_hbm, up_ref))):
@@ -148,6 +152,8 @@
                 )
                 copy.start()
                 copies.append(copy)
+        for copy in sum_copies:
+            copy.start()
         picker = one_hot(slot_ref[...], (cap, slot_ref.shape[1]), 0)
         rows = dot(picker, window_ref[...], ((1,), (0,)))
         squares = as_row(jnp.sum(rows * rows, axis=1, keepdims=True))
@@ -161,8 +167,10 @@
             copy.wait()
         ups = dot(up_ref[...], x_ref[...], ((1,), (1,)))
         if begun:
-            gates = gates + refs[0][...]
-            ups = ups + refs[1][...]
+            for copy in sum_copies:
+                copy.wait()
+            gates = gates + sums[0][...]
+            ups = ups + sums[1][...]
             squares = squares + refs[2][...]
         if last:
             scale = lax.rsqrt(squares * (1.0 / features) + norm_eps)
@@ -179,13 +187,14 @@
     return kernel(
         body,
         result,
-        [SMEM_SPEC, VMEM_SPEC, VMEM_SPEC] + [HBM_SPEC] * 2 + [VMEM_SPEC] * (1 + prior),
+        [SMEM_SPEC, VMEM_SPEC, VMEM_SPEC] + [HBM_SPEC] * 2 + [VMEM_SPEC] + ([HBM_SPEC] * 2 + [VMEM_SPEC]) * (prior > 0),
         [
             pltpu.VMEM((hidden, parts * width), BF16),
             pltpu.VMEM((hidden, parts * width), BF16),
             pltpu.VMEM((cap, parts * width), BF16),
-            pltpu.SemaphoreType.DMA((2 * parts,)),
-        ],
+            pltpu.SemaphoreType.DMA((2 * parts + 2,)),
+        ]
+        + [pltpu.VMEM((hidden, cap), F32)] * (2 if begun else 0),
         56,
     )(positions, slot_lanes, gain, gate, up, window, *(begun or []))
 
@@ -285,17 +294,14 @@
             sum_ref[:, pl.ds(col, block)] = dot(mid, refs[number][...], ((1,), (0,)))
         for number in range(blocks):
             col = pl.multiple_of(pos_ref[count + number], 128)
-            block_sum = sum_ref[:, pl.ds(col, width)]
-            if number < 2:
-                outs[number][...] = block_sum
-            else:
-                rows = slice((number - 2) * tok_dev, (number - 1) * tok_dev)
-                outs[2][rows, :] = block_sum.astype(BF16)
-
-    return kernel(
-        body,
-        [jax.ShapeDtypeStruct((tok_dev, width), F32)] * min(blocks, 2)
-        + [jax.ShapeDtypeStruct(((blocks - 2) * tok_dev, width), BF16)] * (blocks > 2),
+            outs[number][...] = sum_ref[:, pl.ds(col, width)].astype(outs[number].dtype)
+
+    return kernel(
+        body,
+        [
+            jax.ShapeDtypeStruct((tok_dev, width), F32 if n < 2 else BF16)
+            for n in range(blocks)
+        ],
         [SMEM_SPEC] + [VMEM_SPEC] * (3 + count),
         [
             pltpu.VMEM((tok_dev, hidden), F32),
@@ -306,23 +312,23 @@
     )(positions, *begun, *arrays)
 
 
-def finish(shared_own, shared_parts, windows, ids, tok_dev):
+def finish(shared_own, shared_parts, windows, ids, tok_dev, dtype):
     width = shared_own.shape[1]
     parts = len(shared_parts)
 
     def body(own_ref, *refs):
         total = own_ref[...]
         for number in range(parts):
-            total = total + refs[number][:tok_dev, :].astype(F32)
+            total = total + refs[number][...].astype(F32)
         for number in range(len(windows)):
             values, id_ref = refs[parts + number], refs[parts + len(windows) + number]
             picker = one_hot(id_ref[...], (tok_dev, values.shape[0]), 0)
             total = total + dot(picker, values[...], ((1,), (0,)))
-        refs[-1][...] = total.astype(BF16)
-
-    return kernel(
-        body,
-        jax.ShapeDtypeStruct((tok_dev, width), BF16),
+        refs[-1][...] = total.astype(dtype)
+
+    return kernel(
+        body,
+        jax.ShapeDtypeStruct((tok_dev, width), dtype),
         [VMEM_SPEC] * (1 + parts + 2 * len(windows)),
         [],
         54,
@@ -431,7 +437,7 @@
     late_gates, late_ups = shared_gates[6:], shared_ups[6:]
     in_at = feature_at + places(early_gates + early_ups)
     shared_begun = shared_in(token_pieces, early_gates, early_ups, stack_scalars(in_at), gain)
-    masks = [0, 2, 1, 3] if on_line else [0]
+    masks = [0, 2, 3, 1] if on_line else [0]
     out_at = places(late_gates + late_ups + shared_downs)
     out_at += [(tp ^ m) * width for m in masks] if on_line else [0]
     sums = shared_out(
@@ -445,9 +451,9 @@
     )
     if on_line:
         near = swap(sums[2], "tp", 1)
-        half = (sums[1] + near[tok_dev:].astype(F32)).astype(BF16)
+        half = (sums[1] + near.astype(F32)).astype(BF16)
         shared_own = sums[0]
-        shared_parts = [near, swap(half, "tp", 2)]
+        shared_parts = [swap(sums[3], "tp", 1), swap(half, "tp", 2)]
     else:
         shared_own = lax.psum_scatter(sums[0], "tp", scatter_dimension=1, tiled=True)
         shared_parts = []
@@ -465,7 +471,8 @@
         sent = sent.reshape(ep_count, window, width)
         rows = lax.all_to_all(sent, "ep", split_axis=0, concat_axis=0, tiled=True)
         windows.append(rows.reshape(ep_count * window, width))
-    return finish(shared_own, shared_parts, windows, owner_ids, tok_dev)
+    first = finish(shared_own, [], windows[:1], owner_ids[:1], tok_dev, F32)
+    return finish(first, shared_parts, windows[1:], owner_ids[1:], tok_dev, BF16)
 
 
 def solution(mesh):

time: 254 us -> 239 us (0.941)
  waiting for transfers between devices: 125 us -> 112 us
  local copies, waits for them, and re-layouts: 14.6 us -> 11.6 us
    ppermute x29 -> x30, waiting for transfers between devices: 121 us -> 107 us  [swap(): return lax.ppermute(x, axis, [(i, i ^ mask) for i in range(count)])]
    unnamed x60 -> x50, local copies, waits for them, and re-layouts: 9.81 us -> 6.75 us
    pallas_call x2 -> x3, Pallas kernels: 10.5 us -> 12.5 us  [the longest x1 6.99 us: shared_out(): kernel(body, [jax.ShapeDtypeStruct((tok_dev, width), F32 if n < 2 else BF...]
    ppermute x29 -> x30, starting transfers between devices: 42.7 us -> 41.6 us  [swap(): return lax.ppermute(x, axis, [(i, i ^ mask) for i in range(count)])]
  transfers between devices with their start and end apart: 34 -> 35, of which waited for: 9 -> 13; matrix products, arithmetic and copies ran while one was open for 4% -> 4% of each run, Pallas kernels for 15% -> 18%
where the time goes in v3:
time: 239 us; the launch traced here: 238 us
  waiting for transfers between devices  112 us (47%)
  starting transfers between devices  60.9 us (25%)
  Pallas kernels  48.1 us (20%)
  local copies, waits for them, and re-layouts  11.6 us (5%)
  other arithmetic  5.07 us (2%)
    ppermute x30, waiting for transfers between devices, swap(): return lax.ppermute(x, axis, [(i, i ^ mask) for i in range(count)])  107 us
    ppermute x30, starting transfers between devices, swap(): return lax.ppermute(x, axis, [(i, i ^ mask) for i in range(count)])  41.6 us
    all_to_all x4, starting transfers between devices, on_device(): rows = lax.all_to_all(sent, 'ep', split_axis=0, concat_axis=0, tiled=True)  15.5 us
    pallas_call x2, Pallas kernels, expert_hidden(): kernel(body, result, [SMEM_SPEC, VMEM_SPEC, VMEM_SPEC] + [HBM_SPEC] * 2 +...  12.3 us
    pallas_call x2, Pallas kernels, expert_down(): kernel(body, jax.ShapeDtypeStruct((slots, width), BF16), [SMEM_SPEC, VMEM...  9.61 us
    pallas_call x2, Pallas kernels, take_windows(): kernel(body, jax.ShapeDtypeStruct((slots, width * len(pieces)), BF16), [S...  7.16 us
    pallas_call x1, Pallas kernels, shared_out(): kernel(body, [jax.ShapeDtypeStruct((tok_dev, width), F32 if n < 2 else BF...  6.99 us
    unnamed x50, local copies, waits for them, and re-layouts  6.75 us
  transfers between devices with their start and end apart: 35, of which 13 were waited for; matrix products, arithmetic and copies ran while one was open for 4% of the time, Pallas kernels for 18%

profile of v3, /device:TPU:0, one launch (start us, length us, event | category | flops | bytes accessed | tf_op | source)
XLA Modules:
  0.0 238.0 jit_solution(14087959589488589024)
XLA Ops:
  0.0 3.1 %collective-permute-start = (bf16[384,512]{1,0:T(8,128)(2,1)}, bf16[384,512]{1,0:T(8,128)(2,1)S(1)}, u32[]{:S(2)}, u32[]{:S(2)}) collective-permute-start(bf16[384,512]{1,0:T(8,128)(2,1)} %refs_0_.3), channel_id=1, source_target_pairs={{0,8},{8,0},{16,24},{24,16},{1,9},{9,1},{17,25},{25,17},{2,10},{10... | collective-permute-start | bytes 1179656 | tf_op jit(solution)/shard_map/ppermute | solution.py:22
  5.7 3.7 %all-to-all-start = ((s32[8,2,96]{2,1,0:T(2,128)}), s32[8,2,96]{2,1,0:T(2,128)S(1)}, u32[]{:S(2)}, u32[]{:S(2)}) async-start(s32[8,2,96]{2,1,0:T(2,128)} %pad_add_fusion), calls=%async_computation | async-start | bytes 16384 | tf_op jit(solution)/shard_map/all_to_all | solution.py:397
  9.5 4.7 %all-to-all-done = s32[8,2,96]{2,1,0:T(2,128)S(1)} async-done(((s32[8,2,96]{2,1,0:T(2,128)}), s32[8,2,96]{2,1,0:T(2,128)S(1)}, u32[]{:S(2)}, u32[]{:S(2)}) %all-to-all-start) | async-done | bytes 6176 | tf_op jit(solution)/shard_map/all_to_all | solution.py:397
  15.6 3.6 %shard_map.103 = bf16[768,1024]{1,0:T(8,128)(2,1)} custom-call(s32[1]{0:T(128)} %bitcast.12.pos_ref, s32[1,768]{1,0:T(1,128)} %reshape_squeeze.6.ids_ref.refs_1_, bf16[384,512]{1,0:T(8,128)(2,1)} %refs_0_.3, bf16[384,512]{1,0:T(8,128)(2,1)} %copy-done.6), custom_call_target="tpu_custom_call" | custom-call | tf_op jit(solution)/shard_map/pallas_call | solution.py:119
  19.2 3.7 %all-to-all-start.2 = ((bf16[8,96,1024]{2,1,0:T(8,128)(2,1)}), bf16[8,96,1024]{2,1,0:T(8,128)(2,1)S(1)}, u32[]{:S(2)}, u32[]{:S(2)}) async-start(bf16[8,96,1024]{2,1,0:T(8,128)(2,1)} %bitcast.37), calls=%async_computation.2 | async-start | bytes 3145728 | tf_op jit(solution)/shard_map/all_to_all | solution.py:407
  22.9 2.7 %collective-permute-start.1 = (bf16[384,512]{1,0:T(8,128)(2,1)S(1)}, bf16[384,512]{1,0:T(8,128)(2,1)S(1)}, u32[]{:S(2)}, u32[]{:S(2)}) collective-permute-start(bf16[384,512]{1,0:T(8,128)(2,1)S(1)} %copy-done.5), channel_id=1, source_target_pairs={{0,16},{8,24},{16,0},{24,8},{1,17},{9,25},{17,1},{25,9},{2,18},{10... | collective-permute-start | bytes 1179656 | tf_op jit(solution)/shard_map/ppermute | solution.py:22
  25.8 26.2 %collective-permute-done.1.refs_2_.refs_0_ = bf16[384,512]{1,0:T(8,128)(2,1)S(1)} collective-permute-done((bf16[384,512]{1,0:T(8,128)(2,1)S(1)}, bf16[384,512]{1,0:T(8,128)(2,1)S(1)}, u32[]{:S(2)}, u32[]{:S(2)}) %collective-permute-start.1) | collective-permute-done | bytes 393248 | tf_op jit(solution)/shard_map/ppermute | solution.py:22
  53.5 3.6 %shard_map.102 = bf16[768,1024]{1,0:T(8,128)(2,1)} custom-call(s32[1]{0:T(128)} %bitcast.12.pos_ref, s32[1,768]{1,0:T(1,128)} %reshape_squeeze.6.ids_ref.refs_1_, bf16[384,512]{1,0:T(8,128)(2,1)} %copy-done.7, bf16[384,512]{1,0:T(8,128)(2,1)} %copy-done.8), custom_call_target="tpu_custom_call" | custom-call | tf_op jit(solution)/shard_map/pallas_call | solution.py:119
  58.3 3.9 %all-to-all-start.1 = ((bf16[8,96,1024]{2,1,0:T(8,128)(2,1)}), bf16[8,96,1024]{2,1,0:T(8,128)(2,1)S(1)}, u32[]{:S(2)}, u32[]{:S(2)}) async-start(bf16[8,96,1024]{2,1,0:T(8,128)(2,1)} %bitcast.36), calls=%async_computation.1 | async-start | bytes 3145728 | tf_op jit(solution)/shard_map/all_to_all | solution.py:407
  62.1 2.0 collective-permute-start.3
  66.2 24.4 %collective-permute-done.3.refs_5_ = bf16[704,256]{1,0:T(8,128)(2,1)S(1)} collective-permute-done((bf16[704,256]{1,0:T(8,128)(2,1)}, bf16[704,256]{1,0:T(8,128)(2,1)S(1)}, u32[]{:S(2)}, u32[]{:S(2)}) %collective-permute-start.3) | collective-permute-done | bytes 360480 | tf_op jit(solution)/shard_map/ppermute | solution.py:22
  90.6 1.5 collective-permute-start.15
  92.1 1.5 collective-permute-start.17
  93.7 4.8 %collective-permute-done.8.refs_11_ = bf16[704,256]{1,0:T(8,128)(2,1)} collective-permute-done((bf16[704,256]{1,0:T(8,128)(2,1)}, bf16[704,256]{1,0:T(8,128)(2,1)}, u32[]{:S(2)}, u32[]{:S(2)}) %collective-permute-start.8) | collective-permute-done | bytes 360480 | tf_op jit(solution)/shard_map/ppermute | solution.py:22
  101.1 5.9 %collective-permute-done.15.refs_2_ = bf16[704,256]{1,0:T(8,128)(2,1)S(1)} collective-permute-done((bf16[704,256]{1,0:T(8,128)(2,1)}, bf16[704,256]{1,0:T(8,128)(2,1)S(1)}, u32[]{:S(2)}, u32[]{:S(2)}) %collective-permute-start.15) | collective-permute-done | bytes 360480 | tf_op jit(solution)/shard_map/ppermute | solution.py:22
  108.3 5.7 %shard_map.104 = (f32[704,384]{1,0:T(8,128)}, f32[704,384]{1,0:T(8,128)}, f32[1,384]{1,0:T(1,128)}) custom-call(s32[2]{0:T(128)} %pad_add_fusion.3.pos_ref, s32[1,768]{1,0:T(1,128)} %add.120.slot_ref, f32[1,2048]{1,0:T(1,128)} %bitcast.53, bf16[704,2048]{1,0:T(8,128)(2,1)} %bitcast.32, bf16[704,2048]{1,0:T(8,128)(2,1)} %bitcast.34, bf16[768,1024]{1,0:T(8,128)(2,1)} %bitcast.38), custom_call_target="tpu_custom_call" | custom-call | tf_op jit(solution)/shard_map/pallas_call | solution.py:187
  115.2 6.6 %shard_map.105.refs_0_ = bf16[704,384]{1,0:T(8,128)(2,1)} custom-call(s32[2]{0:T(128)} %pad_add_fusion.2.pos_ref, s32[1,768]{1,0:T(1,128)} %add.120.slot_ref, f32[1,2048]{1,0:T(1,128)} %bitcast.54, bf16[704,2048]{1,0:T(8,128)(2,1)} %bitcast.33, bf16[704,2048]{1,0:T(8,128)(2,1)} %bitcast.35, bf16[768,1024]{1,0:T(8,128)(2,1)} %bitcast.39, ...), custom_call_target="tpu_custom_call" | custom-call | tf_op jit(solution)/shard_map/pallas_call | solution.py:187
  121.8 8.2 %collective-permute-start.24 = (bf16[704,384]{1,0:T(8,128)(2,1)}, bf16[704,384]{1,0:T(8,128)(2,1)S(1)}, u32[]{:S(2)}, u32[]{:S(2)}) collective-permute-start(bf16[704,384]{1,0:T(8,128)(2,1)} %shard_map.105.refs_0_), channel_id=1, source_target_pairs={{0,8},{8,0},{16,24},{24,16},{1,9},{9,1},{17,25},{25,17},{2,10},{10... | collective-permute-start | bytes 1622024 | tf_op jit(solution)/shard_map/ppermute | solution.py:22
  133.2 8.0 %collective-permute-done.13.refs_0_ = bf16[704,256]{1,0:T(8,128)(2,1)S(1)} collective-permute-done((bf16[704,256]{1,0:T(8,128)(2,1)}, bf16[704,256]{1,0:T(8,128)(2,1)S(1)}, u32[]{:S(2)}, u32[]{:S(2)}) %collective-permute-start.13) | collective-permute-done | bytes 360480 | tf_op jit(solution)/shard_map/ppermute | solution.py:22
  144.0 4.8 %shard_map.106 = bf16[768,512]{1,0:T(8,128)(2,1)} custom-call(s32[4]{0:T(128)} %pad_add_fusion.1.pos_ref, f32[1,384]{1,0:T(1,128)} %get-tuple-element.34.gate_ref, s32[1,768]{1,0:T(1,128)} %add.120.slot_ref, bf16[2,1408,512]{2,1,0:T(8,128)(2,1)} %down_hbm.3, bf16[704,384]{1,0:T(8,128)(2,1)} %shard_map.105.refs_0_, bf16[704,384]{1,0:T(8,128)(2,1)} %copy-done.12), custom_call_target="tpu_custom_call" | custom-call | tf_op jit(solution)/shard_map/pallas_call | solution.py:221
  148.8 3.9 %all-to-all-start.3 = ((bf16[8,96,512]{2,1,0:T(8,128)(2,1)}), bf16[8,96,512]{2,1,0:T(8,128)(2,1)S(1)}, u32[]{:S(2)}, u32[]{:S(2)}) async-start(bf16[8,96,512]{2,1,0:T(8,128)(2,1)} %bitcast.42), calls=%async_computation.3 | async-start | bytes 1572864 | tf_op jit(solution)/shard_map/all_to_all | solution.py:472
  152.7 2.9 %collective-permute-start.28 = (bf16[704,384]{1,0:T(8,128)(2,1)S(1)}, bf16[704,384]{1,0:T(8,128)(2,1)S(1)}, u32[]{:S(2)}, u32[]{:S(2)}) collective-permute-start(bf16[704,384]{1,0:T(8,128)(2,1)S(1)} %copy-done.4), channel_id=1, source_target_pairs={{0,16},{8,24},{16,0},{24,8},{1,17},{9,25},{17,1},{25,9},{2,18},{10... | collective-permute-start | bytes 1622024 | tf_op jit(solution)/shard_map/ppermute | solution.py:22
  158.2 6.5 %shard_map.100 = (bf16[384,2048]{1,0:T(8,128)(2,1)}, f32[384,704]{1,0:T(8,128)}, f32[384,704]{1,0:T(8,128)}) custom-call(s32[17]{0:T(128)} %stack.124.pos_ref, f32[1,2048]{1,0:T(1,128)} %bitcast.55, bf16[384,512]{1,0:T(8,128)(2,1)} %refs_0_.3, bf16[384,512]{1,0:T(8,128)(2,1)} %copy-done.6, bf16[384,512]{1,0:T(8,128)(2,1)} %copy-done.7, ...), custom_call_target="tpu_custom_call" | custom-call | tf_op jit(solution)/shard_map/pallas_call | solution.py:262
  164.7 7.0 %shard_map.101 = (f32[384,512]{1,0:T(8,128)}, f32[384,512]{1,0:T(8,128)}, bf16[384,512]{1,0:T(8,128)(2,1)}, bf16[384,512]{1,0:T(8,128)(2,1)}) custom-call(s32[16]{0:T(128)} %stack.121.pos_ref, bf16[384,2048]{1,0:T(8,128)(2,1)} %get-tuple-element.15.x_ref, f32[384,704]{1,0:T(8,128)} %get-tuple-element.16.gate_in, f32[384,704]{1,0:T(8,128)} %get-tuple-element.17.up_in, ...), custom_call_target="tpu_custom_call" | custom-call | tf_op jit(solution)/shard_map/pallas_call | solution.py:299
  172.9 19.1 %collective-permute-done.28.refs_0_ = bf16[704,384]{1,0:T(8,128)(2,1)S(1)} collective-permute-done((bf16[704,384]{1,0:T(8,128)(2,1)S(1)}, bf16[704,384]{1,0:T(8,128)(2,1)S(1)}, u32[]{:S(2)}, u32[]{:S(2)}) %collective-permute-start.28) | collective-permute-done | bytes 540704 | tf_op jit(solution)/shard_map/ppermute | solution.py:22
  193.0 4.8 %shard_map.108 = bf16[768,512]{1,0:T(8,128)(2,1)} custom-call(s32[4]{0:T(128)} %pad_add_fusion.4.pos_ref, f32[1,384]{1,0:T(1,128)} %get-tuple-element.33.gate_ref, s32[1,768]{1,0:T(1,128)} %add.132.slot_ref, bf16[2,1408,512]{2,1,0:T(8,128)(2,1)} %down_hbm.3, bf16[704,384]{1,0:T(8,128)(2,1)} %copy-done.10, bf16[704,384]{1,0:T(8,128)(2,1)} %copy-done.11), custom_call_target="tpu_custom_call" | custom-call | tf_op jit(solution)/shard_map/pallas_call | solution.py:221
  197.9 4.1 %all-to-all-start.4 = ((bf16[8,96,512]{2,1,0:T(8,128)(2,1)}), bf16[8,96,512]{2,1,0:T(8,128)(2,1)S(1)}, u32[]{:S(2)}, u32[]{:S(2)}) async-start(bf16[8,96,512]{2,1,0:T(8,128)(2,1)} %bitcast.43), calls=%async_computation.4 | async-start | bytes 1572864 | tf_op jit(solution)/shard_map/all_to_all | solution.py:472
  202.0 11.4 %collective-permute-start.25 = (bf16[384,512]{1,0:T(8,128)(2,1)}, bf16[384,512]{1,0:T(8,128)(2,1)}, u32[]{:S(2)}, u32[]{:S(2)}) collective-permute-start(bf16[384,512]{1,0:T(8,128)(2,1)} %get-tuple-element.22), channel_id=1, source_target_pairs={{0,8},{8,0},{16,24},{24,16},{1,9},{9,1},{17,25},{25,17},{2,10},{10... | collective-permute-start | bytes 1179656 | tf_op jit(solution)/shard_map/ppermute | solution.py:22
  215.1 2.7 %shard_map.107.own_ref = f32[384,512]{1,0:T(8,128)} custom-call(f32[384,512]{1,0:T(8,128)} %get-tuple-element.18.own_ref, bf16[768,512]{1,0:T(8,128)(2,1)} %bitcast.40, s32[1,768]{1,0:T(1,128)} %reshape_squeeze.6.ids_ref.refs_1_), custom_call_target="tpu_custom_call" | custom-call | tf_op jit(solution)/shard_map/pallas_call | solution.py:329
  217.9 13.8 %collective-permute-done.25.refs_0_ = bf16[384,512]{1,0:T(8,128)(2,1)} collective-permute-done((bf16[384,512]{1,0:T(8,128)(2,1)}, bf16[384,512]{1,0:T(8,128)(2,1)}, u32[]{:S(2)}, u32[]{:S(2)}) %collective-permute-start.25) | collective-permute-done | bytes 393248 | tf_op jit(solution)/shard_map/ppermute | solution.py:22
  231.6 2.5 %collective-permute-done.27.refs_1_ = bf16[384,512]{1,0:T(8,128)(2,1)S(1)} collective-permute-done((bf16[384,512]{1,0:T(8,128)(2,1)S(1)}, bf16[384,512]{1,0:T(8,128)(2,1)S(1)}, u32[]{:S(2)}, u32[]{:S(2)}) %collective-permute-start.27) | collective-permute-done | bytes 393248 | tf_op jit(solution)/shard_map/ppermute | solution.py:22
  235.2 2.8 %shard_map.109 = bf16[384,512]{1,0:T(8,128)(2,1)} custom-call(f32[384,512]{1,0:T(8,128)} %shard_map.107.own_ref, bf16[384,512]{1,0:T(8,128)(2,1)} %collective-permute-done.25.refs_0_, bf16[384,512]{1,0:T(8,128)(2,1)} %copy-done.13, bf16[768,512]{1,0:T(8,128)(2,1)} %bitcast.41, s32[1,768]{1,0:T(1,128)} %reshape_squeeze.7.refs_3_), custom_call_target="tpu_custom_call" | custom-call | tf_op jit(solution)/shard_map/pallas_call | solution.py:329
  (125 shorter events, 27.7 us)
Async XLA Ops:
  0.0 14.9 %collective-permute-start = (bf16[384,512]{1,0:T(8,128)(2,1)}, bf16[384,512]{1,0:T(8,128)(2,1)S(1)}, u32[]{:S(2)}, u32[]{:S(2)}) collective-permute-start(bf16[384,512]{1,0:T(8,128)(2,1)} %refs_0_.3), channel_id=1, source_target_pairs={{0,8},{8,0},{16,24},{24,16},{1,9},{9,1},{17,25},{25,17},{2,10},{10... | collective-permute-start | bytes 1179656 | tf_op jit(solution)/shard_map/ppermute | solution.py:22
  19.2 37.9 %all-to-all-start.2 = ((bf16[8,96,1024]{2,1,0:T(8,128)(2,1)}), bf16[8,96,1024]{2,1,0:T(8,128)(2,1)S(1)}, u32[]{:S(2)}, u32[]{:S(2)}) async-start(bf16[8,96,1024]{2,1,0:T(8,128)(2,1)} %bitcast.37), calls=%async_computation.2 | async-start | bytes 3145728 | tf_op jit(solution)/shard_map/all_to_all | solution.py:407
  22.9 29.1 %collective-permute-start.1 = (bf16[384,512]{1,0:T(8,128)(2,1)S(1)}, bf16[384,512]{1,0:T(8,128)(2,1)S(1)}, u32[]{:S(2)}, u32[]{:S(2)}) collective-permute-start(bf16[384,512]{1,0:T(8,128)(2,1)S(1)} %copy-done.5), channel_id=1, source_target_pairs={{0,16},{8,24},{16,0},{24,8},{1,17},{9,25},{17,1},{25,9},{2,18},{10... | collective-permute-start | bytes 1179656 | tf_op jit(solution)/shard_map/ppermute | solution.py:22
  25.6 26.5 %collective-permute-start.2 = (bf16[384,512]{1,0:T(8,128)(2,1)S(1)}, bf16[384,512]{1,0:T(8,128)(2,1)S(1)}, u32[]{:S(2)}, u32[]{:S(2)}) collective-permute-start(bf16[384,512]{1,0:T(8,128)(2,1)S(1)} %copy-done.5), channel_id=1, source_target_pairs={{0,24},{8,16},{16,8},{24,0},{1,25},{9,17},{17,9},{25,1},{2,26},{10... | collective-permute-start | bytes 1179656 | tf_op jit(solution)/shard_map/ppermute | solution.py:22
  58.3 55.7 %all-to-all-start.1 = ((bf16[8,96,1024]{2,1,0:T(8,128)(2,1)}), bf16[8,96,1024]{2,1,0:T(8,128)(2,1)S(1)}, u32[]{:S(2)}, u32[]{:S(2)}) async-start(bf16[8,96,1024]{2,1,0:T(8,128)(2,1)} %bitcast.36), calls=%async_computation.1 | async-start | bytes 3145728 | tf_op jit(solution)/shard_map/all_to_all | solution.py:407
  62.1 28.4 %collective-permute-start.3 = (bf16[704,256]{1,0:T(8,128)(2,1)}, bf16[704,256]{1,0:T(8,128)(2,1)S(1)}, u32[]{:S(2)}, u32[]{:S(2)}) collective-permute-start(bf16[704,256]{1,0:T(8,128)(2,1)} %bitcast.44), channel_id=1, source_target_pairs={{0,2},{1,3},{2,0},{3,1},{4,6},{5,7},{6,4},{7,5},{8,10},{9,11},{10,... | collective-permute-start | bytes 1081352 | tf_op jit(solution)/shard_map/ppermute | solution.py:22
  64.2 26.4 %collective-permute-start.4 = (bf16[704,256]{1,0:T(8,128)(2,1)}, bf16[704,256]{1,0:T(8,128)(2,1)}, u32[]{:S(2)}, u32[]{:S(2)}) collective-permute-start(bf16[704,256]{1,0:T(8,128)(2,1)} %bitcast.45), channel_id=1, source_target_pairs={{0,4},{1,5},{2,6},{3,7},{4,0},{5,1},{6,2},{7,3},{8,12},{9,13},{10,... | collective-permute-start | bytes 1081352 | tf_op jit(solution)/shard_map/ppermute | solution.py:22
  65.6 26.5 %collective-permute-start.5 = (bf16[704,256]{1,0:T(8,128)(2,1)}, bf16[704,256]{1,0:T(8,128)(2,1)S(1)}, u32[]{:S(2)}, u32[]{:S(2)}) collective-permute-start(bf16[704,256]{1,0:T(8,128)(2,1)} %bitcast.46), channel_id=1, source_target_pairs={{0,1},{1,0},{2,3},{3,2},{4,5},{5,4},{6,7},{7,6},{8,9},{9,8},{10,11... | collective-permute-start | bytes 1081352 | tf_op jit(solution)/shard_map/ppermute | solution.py:22
  65.6 32.8 %collective-permute-start.8 = (bf16[704,256]{1,0:T(8,128)(2,1)}, bf16[704,256]{1,0:T(8,128)(2,1)}, u32[]{:S(2)}, u32[]{:S(2)}) collective-permute-start(bf16[704,256]{1,0:T(8,128)(2,1)} %bitcast.48), channel_id=1, source_target_pairs={{0,2},{1,3},{2,0},{3,1},{4,6},{5,7},{6,4},{7,5},{8,10},{9,11},{10,... | collective-permute-start | bytes 1081352 | tf_op jit(solution)/shard_map/ppermute | solution.py:22
  66.2 33.7 %collective-permute-start.9 = (bf16[704,256]{1,0:T(8,128)(2,1)}, bf16[704,256]{1,0:T(8,128)(2,1)}, u32[]{:S(2)}, u32[]{:S(2)}) collective-permute-start(bf16[704,256]{1,0:T(8,128)(2,1)} %bitcast.49), channel_id=1, source_target_pairs={{0,4},{1,5},{2,6},{3,7},{4,0},{5,1},{6,2},{7,3},{8,12},{9,13},{10,... | collective-permute-start | bytes 1081352 | tf_op jit(solution)/shard_map/ppermute | solution.py:22
  90.6 10.0 %collective-permute-start.10 = (bf16[704,256]{1,0:T(8,128)(2,1)}, bf16[704,256]{1,0:T(8,128)(2,1)}, u32[]{:S(2)}, u32[]{:S(2)}) collective-permute-start(bf16[704,256]{1,0:T(8,128)(2,1)} %bitcast.50), channel_id=1, source_target_pairs={{0,1},{1,0},{2,3},{3,2},{4,5},{5,4},{6,7},{7,6},{8,9},{9,8},{10,11... | collective-permute-start | bytes 1081352 | tf_op jit(solution)/shard_map/ppermute | solution.py:22
  90.6 16.4 %collective-permute-start.15 = (bf16[704,256]{1,0:T(8,128)(2,1)}, bf16[704,256]{1,0:T(8,128)(2,1)S(1)}, u32[]{:S(2)}, u32[]{:S(2)}) collective-permute-start(bf16[704,256]{1,0:T(8,128)(2,1)} %bitcast.51), channel_id=1, source_target_pairs={{0,6},{1,7},{2,4},{3,5},{4,2},{5,3},{6,0},{7,1},{8,14},{9,15},{10,... | collective-permute-start | bytes 1081352 | tf_op jit(solution)/shard_map/ppermute | solution.py:22
  92.1 29.7 %collective-permute-start.17 = (bf16[704,256]{1,0:T(8,128)(2,1)S(1)}, bf16[704,256]{1,0:T(8,128)(2,1)S(1)}, u32[]{:S(2)}, u32[]{:S(2)}) collective-permute-start(bf16[704,256]{1,0:T(8,128)(2,1)S(1)} %copy-done.14), channel_id=1, source_target_pairs={{0,2},{1,3},{2,0},{3,1},{4,6},{5,7},{6,4},{7,5},{8,10},{9,11},{10,... | collective-permute-start | bytes 1081352 | tf_op jit(solution)/shard_map/ppermute | solution.py:22
  98.4 31.6 %collective-permute-start.18 = (bf16[704,256]{1,0:T(8,128)(2,1)S(1)}, bf16[704,256]{1,0:T(8,128)(2,1)}, u32[]{:S(2)}, u32[]{:S(2)}) collective-permute-start(bf16[704,256]{1,0:T(8,128)(2,1)S(1)} %copy-done.14), channel_id=1, source_target_pairs={{0,4},{1,5},{2,6},{3,7},{4,0},{5,1},{6,2},{7,3},{8,12},{9,13},{10,... | collective-permute-start | bytes 1081352 | tf_op jit(solution)/shard_map/ppermute | solution.py:22
  99.9 30.4 %collective-permute-start.19 = (bf16[704,256]{1,0:T(8,128)(2,1)S(1)}, bf16[704,256]{1,0:T(8,128)(2,1)S(1)}, u32[]{:S(2)}, u32[]{:S(2)}) collective-permute-start(bf16[704,256]{1,0:T(8,128)(2,1)S(1)} %copy-done.14), channel_id=1, source_target_pairs={{0,1},{1,0},{2,3},{3,2},{4,5},{5,4},{6,7},{7,6},{8,9},{9,8},{10,11... | collective-permute-start | bytes 1081352 | tf_op jit(solution)/shard_map/ppermute | solution.py:22
  100.6 30.0 %collective-permute-start.6 = (bf16[704,256]{1,0:T(8,128)(2,1)S(1)}, bf16[704,256]{1,0:T(8,128)(2,1)}, u32[]{:S(2)}, u32[]{:S(2)}) collective-permute-start(bf16[704,256]{1,0:T(8,128)(2,1)S(1)} %collective-permute-done.3.refs_5_), channel_id=1, source_target_pairs={{0,1},{1,0},{2,3},{3,2},{4,5},{5,4},{6,7},{7,6},{8,9},{9,8},{10,11... | collective-permute-start | bytes 1081352 | tf_op jit(solution)/shard_map/ppermute | solution.py:22
  107.0 24.2 %collective-permute-start.7 = (bf16[704,256]{1,0:T(8,128)(2,1)}, bf16[704,256]{1,0:T(8,128)(2,1)}, u32[]{:S(2)}, u32[]{:S(2)}) collective-permute-start(bf16[704,256]{1,0:T(8,128)(2,1)} %collective-permute-done.4.refs_6_), channel_id=1, source_target_pairs={{0,1},{1,0},{2,3},{3,2},{4,5},{5,4},{6,7},{7,6},{8,9},{9,8},{10,11... | collective-permute-start | bytes 1081352 | tf_op jit(solution)/shard_map/ppermute | solution.py:22
  121.8 21.3 %collective-permute-start.24 = (bf16[704,384]{1,0:T(8,128)(2,1)}, bf16[704,384]{1,0:T(8,128)(2,1)S(1)}, u32[]{:S(2)}, u32[]{:S(2)}) collective-permute-start(bf16[704,384]{1,0:T(8,128)(2,1)} %shard_map.105.refs_0_), channel_id=1, source_target_pairs={{0,8},{8,0},{16,24},{24,16},{1,9},{9,1},{17,25},{25,17},{2,10},{10... | collective-permute-start | bytes 1622024 | tf_op jit(solution)/shard_map/ppermute | solution.py:22
  130.6 10.7 %collective-permute-start.13 = (bf16[704,256]{1,0:T(8,128)(2,1)}, bf16[704,256]{1,0:T(8,128)(2,1)S(1)}, u32[]{:S(2)}, u32[]{:S(2)}) collective-permute-start(bf16[704,256]{1,0:T(8,128)(2,1)} %collective-permute-done.4.refs_6_), channel_id=1, source_target_pairs={{0,2},{1,3},{2,0},{3,1},{4,6},{5,7},{6,4},{7,5},{8,10},{9,11},{10,... | collective-permute-start | bytes 1081352 | tf_op jit(solution)/shard_map/ppermute | solution.py:22
  131.1 10.3 %collective-permute-start.22 = (bf16[704,256]{1,0:T(8,128)(2,1)S(1)}, bf16[704,256]{1,0:T(8,128)(2,1)}, u32[]{:S(2)}, u32[]{:S(2)}) collective-permute-start(bf16[704,256]{1,0:T(8,128)(2,1)S(1)} %collective-permute-done.17.refs_5_), channel_id=1, source_target_pairs={{0,4},{1,5},{2,6},{3,7},{4,0},{5,1},{6,2},{7,3},{8,12},{9,13},{10,... | collective-permute-start | bytes 1081352 | tf_op jit(solution)/shard_map/ppermute | solution.py:22
  131.9 23.7 %collective-permute-start.20 = (bf16[704,256]{1,0:T(8,128)(2,1)S(1)}, bf16[704,256]{1,0:T(8,128)(2,1)}, u32[]{:S(2)}, u32[]{:S(2)}) collective-permute-start(bf16[704,256]{1,0:T(8,128)(2,1)S(1)} %collective-permute-done.17.refs_5_), channel_id=1, source_target_pairs={{0,1},{1,0},{2,3},{3,2},{4,5},{5,4},{6,7},{7,6},{8,9},{9,8},{10,11... | collective-permute-start | bytes 1081352 | tf_op jit(solution)/shard_map/ppermute | solution.py:22
  132.5 20.2 %collective-permute-start.16 = (bf16[704,256]{1,0:T(8,128)(2,1)S(1)}, bf16[704,256]{1,0:T(8,128)(2,1)S(1)}, u32[]{:S(2)}, u32[]{:S(2)}) collective-permute-start(bf16[704,256]{1,0:T(8,128)(2,1)S(1)} %collective-permute-done.15.refs_2_), channel_id=1, source_target_pairs={{0,1},{1,0},{2,3},{3,2},{4,5},{5,4},{6,7},{7,6},{8,9},{9,8},{10,11... | collective-permute-start | bytes 1081352 | tf_op jit(solution)/shard_map/ppermute | solution.py:22
  141.3 23.4 %collective-permute-start.21 = (bf16[704,256]{1,0:T(8,128)(2,1)}, bf16[704,256]{1,0:T(8,128)(2,1)}, u32[]{:S(2)}, u32[]{:S(2)}) collective-permute-start(bf16[704,256]{1,0:T(8,128)(2,1)} %collective-permute-done.18.refs_6_), channel_id=1, source_target_pairs={{0,1},{1,0},{2,3},{3,2},{4,5},{5,4},{6,7},{7,6},{8,9},{9,8},{10,11... | collective-permute-start | bytes 1081352 | tf_op jit(solution)/shard_map/ppermute | solution.py:22
  141.5 23.2 %collective-permute-start.14 = (bf16[704,256]{1,0:T(8,128)(2,1)S(1)}, bf16[704,256]{1,0:T(8,128)(2,1)}, u32[]{:S(2)}, u32[]{:S(2)}) collective-permute-start(bf16[704,256]{1,0:T(8,128)(2,1)S(1)} %collective-permute-done.13.refs_0_), channel_id=1, source_target_pairs={{0,1},{1,0},{2,3},{3,2},{4,5},{5,4},{6,7},{7,6},{8,9},{9,8},{10,11... | collective-permute-start | bytes 1081352 | tf_op jit(solution)/shard_map/ppermute | solution.py:22
  143.2 21.5 %collective-permute-start.23 = (bf16[704,256]{1,0:T(8,128)(2,1)}, bf16[704,256]{1,0:T(8,128)(2,1)}, u32[]{:S(2)}, u32[]{:S(2)}) collective-permute-start(bf16[704,256]{1,0:T(8,128)(2,1)} %collective-permute-done.22.refs_10_), channel_id=1, source_target_pairs={{0,1},{1,0},{2,3},{3,2},{4,5},{5,4},{6,7},{7,6},{8,9},{9,8},{10,11... | collective-permute-start | bytes 1081352 | tf_op jit(solution)/shard_map/ppermute | solution.py:22
  148.8 49.1 %all-to-all-start.3 = ((bf16[8,96,512]{2,1,0:T(8,128)(2,1)}), bf16[8,96,512]{2,1,0:T(8,128)(2,1)S(1)}, u32[]{:S(2)}, u32[]{:S(2)}) async-start(bf16[8,96,512]{2,1,0:T(8,128)(2,1)} %bitcast.42), calls=%async_computation.3 | async-start | bytes 1572864 | tf_op jit(solution)/shard_map/all_to_all | solution.py:472
  152.7 39.3 %collective-permute-start.28 = (bf16[704,384]{1,0:T(8,128)(2,1)S(1)}, bf16[704,384]{1,0:T(8,128)(2,1)S(1)}, u32[]{:S(2)}, u32[]{:S(2)}) collective-permute-start(bf16[704,384]{1,0:T(8,128)(2,1)S(1)} %copy-done.4), channel_id=1, source_target_pairs={{0,16},{8,24},{16,0},{24,8},{1,17},{9,25},{17,1},{25,9},{2,18},{10... | collective-permute-start | bytes 1622024 | tf_op jit(solution)/shard_map/ppermute | solution.py:22
  155.7 36.4 %collective-permute-start.29 = (bf16[704,384]{1,0:T(8,128)(2,1)S(1)}, bf16[704,384]{1,0:T(8,128)(2,1)S(1)}, u32[]{:S(2)}, u32[]{:S(2)}) collective-permute-start(bf16[704,384]{1,0:T(8,128)(2,1)S(1)} %copy-done.4), channel_id=1, source_target_pairs={{0,24},{8,16},{16,8},{24,0},{1,25},{9,17},{17,9},{25,1},{2,26},{10... | collective-permute-start | bytes 1622024 | tf_op jit(solution)/shard_map/ppermute | solution.py:22
  171.7 41.7 %collective-permute-start.26 = (bf16[384,512]{1,0:T(8,128)(2,1)}, bf16[384,512]{1,0:T(8,128)(2,1)S(1)}, u32[]{:S(2)}, u32[]{:S(2)}) collective-permute-start(bf16[384,512]{1,0:T(8,128)(2,1)} %get-tuple-element.24), channel_id=1, source_target_pairs={{0,8},{8,0},{16,24},{24,16},{1,9},{9,1},{17,25},{25,17},{2,10},{10... | collective-permute-start | bytes 1179656 | tf_op jit(solution)/shard_map/ppermute | solution.py:22
  197.9 36.3 %all-to-all-start.4 = ((bf16[8,96,512]{2,1,0:T(8,128)(2,1)}), bf16[8,96,512]{2,1,0:T(8,128)(2,1)S(1)}, u32[]{:S(2)}, u32[]{:S(2)}) async-start(bf16[8,96,512]{2,1,0:T(8,128)(2,1)} %bitcast.43), calls=%async_computation.4 | async-start | bytes 1572864 | tf_op jit(solution)/shard_map/all_to_all | solution.py:472
  202.0 29.7 %collective-permute-start.25 = (bf16[384,512]{1,0:T(8,128)(2,1)}, bf16[384,512]{1,0:T(8,128)(2,1)}, u32[]{:S(2)}, u32[]{:S(2)}) collective-permute-start(bf16[384,512]{1,0:T(8,128)(2,1)} %get-tuple-element.22), channel_id=1, source_target_pairs={{0,8},{8,0},{16,24},{24,16},{1,9},{9,1},{17,25},{25,17},{2,10},{10... | collective-permute-start | bytes 1179656 | tf_op jit(solution)/shard_map/ppermute | solution.py:22
  213.5 20.7 %collective-permute-start.27 = (bf16[384,512]{1,0:T(8,128)(2,1)S(1)}, bf16[384,512]{1,0:T(8,128)(2,1)S(1)}, u32[]{:S(2)}, u32[]{:S(2)}) collective-permute-start(bf16[384,512]{1,0:T(8,128)(2,1)S(1)} %add_convert_fusion), channel_id=1, source_target_pairs={{0,16},{8,24},{16,0},{24,8},{1,17},{9,25},{17,1},{25,9},{2,18},{10... | collective-permute-start | bytes 1179656 | tf_op jit(solution)/shard_map/ppermute | solution.py:22
  (28 other events, 284.3 us)
